TPU v7x, 32 devices: a whole 2x2x4 slice. The times are simulated.
32 devices in a mesh: det: 8 (over y, x, core), bm: 4 (over z).
Axes of the slice: x: 2, y: 2, z: 4, core: 2. Of those that a mesh axis runs over, the one named last changes fastest.
Arguments:
- sky_alm: bfloat16 [2, 3, 16, 128], P(None, None, 'det'), may hold values from -6 to 6
- beam_blm: bfloat16 [2, 3, 16, 128], P(None, None, 'bm'), may hold values from -2.5 to 2.5
- wigner: bfloat16 [32, 16, 16, 128], P('det', None, 'bm'), may hold values from -0.03125 to 0.03125
- theta_index: int32 [128, 256], P('det'), may hold values from 0 to 3
- phi_index: int32 [128, 256], P('det'), may hold values from 0 to 16383
- psi_index: int32 [128, 256], P('det'), may hold values from 0 to 31
Outputs:
- tod: float32 [128, 256], P('det', 'bm')
All inputs are finite; a program needn't handle non-finite values.
Results may differ from a plain program's by a relative error of at most 0.0029.
Values may be sent and summed in bfloat16 or wider, within the bound.
No kernel may reach another device: no remote copies, remote signals or barrier semaphores. Data moves between devices by JAX's collectives and lax.ppermute only.
A program may use at most 64 MiB of HBM per device.

v0:
```python
import math

import jax
import jax.numpy as jnp
from jax import lax
from jax.sharding import PartitionSpec as P

NPHI = 16384
NPSI = 32


TWO_PI = 2.0 * math.pi


def spectra_of(sky, beam):
    sky_full = sky.astype(jnp.float32)[:, :, :, None, :]
    beam_full = beam.astype(jnp.float32)[:, :, None, :, :]
    real_part = jnp.sum(sky_full[0] * beam_full[0] - sky_full[1] * beam_full[1], axis=0)
    imag_part = jnp.sum(sky_full[0] * beam_full[1] + sky_full[1] * beam_full[0], axis=0)
    return jnp.stack([real_part, imag_part]).astype(jnp.bfloat16)


def contract(table, spectra):
    return jnp.einsum("rmpl,kmpl->krpm", table, spectra, preferred_element_type=jnp.float32)


def product_first(left, right):
    dims = (((0,), (0,)), ((), ()))
    return lax.dot_general(
        left, right, dims, precision=lax.Precision.HIGHEST, preferred_element_type=jnp.float32
    )


def sample_tod(cube, theta, phi, psi):
    cycles = cube.shape[1]
    planes = cube.shape[2]
    modes = cube.shape[3]
    plane_ids = jnp.arange(planes, dtype=jnp.int32)
    psi_angle = TWO_PI * (plane_ids[:, None] * psi[None, :] % NPSI).astype(jnp.float32) / NPSI
    select = (theta[None, :] == jnp.arange(cycles, dtype=jnp.int32)[:, None]).astype(jnp.float32)
    cos_feat = (select[:, None, :] * jnp.cos(psi_angle)[None]).reshape(cycles * planes, -1)
    sin_feat = (select[:, None, :] * jnp.sin(psi_angle)[None]).reshape(cycles * planes, -1)
    flat = cube.reshape(2, cycles * planes, modes)
    k_real = product_first(flat[0], cos_feat) - product_first(flat[1], sin_feat)
    k_imag = product_first(flat[1], cos_feat) + product_first(flat[0], sin_feat)
    mode_ids = jnp.arange(modes, dtype=jnp.int32)
    phi_angle = TWO_PI * (mode_ids[:, None] * phi[None, :] % NPHI).astype(jnp.float32) / NPHI
    return jnp.sum(k_real * jnp.cos(phi_angle) - k_imag * jnp.sin(phi_angle), axis=0)


def on_device(sky_alm, beam_blm, wigner, theta_index, phi_index, psi_index):
    cube = contract(
        wigner, spectra_of(lax.all_gather(sky_alm, "det", axis=2, tiled=True), beam_blm)
    )
    all_planes = lax.all_gather(cube, "bm", axis=2, tiled=True)
    width = theta_index.shape[1] // lax.axis_size("bm")
    offset = lax.axis_index("bm") * width

    def columns(values):
        return lax.dynamic_slice_in_dim(values, offset, width, 1).reshape(-1)

    result = sample_tod(all_planes, columns(theta_index), columns(phi_index), columns(psi_index))
    return result.reshape(theta_index.shape[0], width)


def solution(mesh):
    placed = (
        P(None, None, "det", None),
        P(None, None, "bm", None),
        P("det", None, "bm", None),
        P("det", None),
        P("det", None),
        P("det", None),
    )
    return jax.shard_map(
        on_device, mesh=mesh, in_specs=placed, out_specs=P("det", "bm"), check_vma=False
    )
```

profile of v0, /device:TPU:0, one launch (start us, length us, event | category | flops | bytes accessed | tf_op | source)
XLA Modules:
  0.0 30.0 jit_solution(16744482656329492623)
XLA Ops:
  0.0 0.0 copy-start
  0.0 0.8 %constant_dynamic-slice_fusion = (s32[16,64]{1,0:T(8,128)S(1)}, s32[16,64]{1,0:T(8,128)S(1)}) fusion(s32[16,256]{1,0:T(8,128)} %param.10, s32[]{:T(128)S(6)} %select_n.23, s32[16,256]{1,0:T(8,128)} %param.11), kind=kLoop, calls=%fused_computation.43 | loop fusion | bytes 16388 | tf_op jit(solution)/shard_map/dynamic_slice | solution.py:60
  0.8 0.1 mul.167
  0.9 0.0 copy-start.2
  0.9 0.3 fusion.18
  1.2 0.4 %copy-done.2 = s32[16,256]{1,0:T(8,128)S(1)} copy-done((s32[16,256]{1,0:T(8,128)S(1)}, s32[16,256]{1,0:T(8,128)}, u32[]{:S(2)}) %copy-start.2) | copy-done | bytes 16408
  1.6 0.1 constant_dynamic-slice_fusion.2
  1.7 0.1 eq.22
  1.8 0.0 copy-start.3
  1.8 0.7 %copy-done.3 = bf16[2,3,2,128]{3,2,1,0:T(2,128)(2,1)S(1)} copy-done((bf16[2,3,2,128]{3,2,1,0:T(2,128)(2,1)S(1)}, bf16[2,3,2,128]{3,2,1,0:T(2,128)(2,1)}, u32[]{:S(2)}) %copy-start.3) | copy-done | bytes 3096
  2.5 10.6 %all_gather.6 = bf16[2,3,16,128]{3,0,1,2:T(2,128)(2,1)S(1)} all-gather(bf16[2,3,2,128]{3,0,1,2:T(2,128)(2,1)S(1)} %copy.30), channel_id=1, replica_groups=mesh['det'=8,'bm'=4] {'det'}, dimensions={2}, use_global_device_ids=true | all-gather | bytes 27648 | tf_op jit(solution)/shard_map/all_gather | solution.py:53
  13.1 0.0 copy-start.1
  13.1 0.7 %copy-done.1 = bf16[2,3,4,128]{3,2,1,0:T(4,128)(2,1)S(1)} copy-done((bf16[2,3,4,128]{3,2,1,0:T(4,128)(2,1)S(1)}, bf16[2,3,4,128]{3,2,1,0:T(4,128)(2,1)}, u32[]{:S(2)}) %copy-start.1) | copy-done | bytes 6168
  13.9 0.0 copy-done
  13.9 0.2 convolution_bitcast_fusion
  14.1 0.1 copy.35
  14.3 13.3 %all_gather.7 = f32[2,4,16,16]{3,1,0,2:T(4,128)S(1)} all-gather(f32[2,4,4,16]{3,1,0,2:T(4,128)S(1)} %copy.35), channel_id=1, replica_groups=mesh['det'=8,'bm'=4] {'bm'}, dimensions={2}, use_global_device_ids=true | all-gather | bytes 10240 | tf_op jit(solution)/shard_map/all_gather | solution.py:55
  27.6 0.1 copy.37
  27.7 0.1 squeeze.5
  27.8 0.3 fusion.24
  28.0 0.1 copy.36
  28.1 0.1 squeeze.4
  28.2 0.1 mul.177
  28.3 0.4 %fusion.2 = f32[16,1024]{1,0:T(8,128)S(1)} fusion(f32[16,1024]{1,0:T(8,128)S(1)} %fusion.24, f32[64,16]{0,1:T(8,128)S(1)} %squeeze.4, f32[64,1024]{1,0:T(8,128)S(1)} %bitcast.30, s32[1024]{0:T(1024)S(1)} %mul.177), kind=kOutput, calls=%fused_computation.5 | convolution fusion | flops 12845056 | bytes 401408 | tf_op jit(solution)/shard_map/dot_general | solution.py:29
  28.7 0.3 fusion.23
  28.9 0.4 %fusion.3 = f32[1024]{0:T(1024)S(1)} fusion(f32[16,1024]{1,0:T(8,128)S(1)} %fusion.2, f32[16,1024]{1,0:T(8,128)S(1)} %fusion.23, f32[64,16]{0,1:T(8,128)S(1)} %squeeze.5, f32[64,1024]{1,0:T(8,128)S(1)} %bitcast.31, s32[1024]{0:T(1024)S(1)} %mul.177), kind=kOutput, calls=%fused_computation.6 | convolution fusion | flops 12876800 | bytes 405504 | tf_op jit(solution)/shard_map/dot_general | solution.py:29
  29.3 0.7 %reshape.136 = f32[16,64]{1,0:T(8,128)} reshape(f32[1024]{0:T(1024)S(1)} %fusion.3) | data formatting | bytes 8192 | tf_op jit(solution)/shard_map/reshape | solution.py:63
  (11 shorter events, 0.2 us)
Async XLA Ops:
  0.0 13.9 %copy-start = (bf16[4,16,4,128]{3,2,1,0:T(4,128)(2,1)S(1)}, bf16[4,16,4,128]{3,2,1,0:T(4,128)(2,1)}, u32[]{:S(2)}) copy-start(bf16[4,16,4,128]{3,2,1,0:T(4,128)(2,1)} %param.8) | copy-start | bytes 196612
  0.9 0.7 %copy-start.2 = (s32[16,256]{1,0:T(8,128)S(1)}, s32[16,256]{1,0:T(8,128)}, u32[]{:S(2)}) copy-start(s32[16,256]{1,0:T(8,128)} %param.9) | copy-start | bytes 49156
  1.8 0.7 %copy-start.3 = (bf16[2,3,2,128]{3,2,1,0:T(2,128)(2,1)S(1)}, bf16[2,3,2,128]{3,2,1,0:T(2,128)(2,1)}, u32[]{:S(2)}) copy-start(bf16[2,3,2,128]{3,2,1,0:T(2,128)(2,1)} %param.6) | copy-start | bytes 9220
  13.1 0.7 %copy-start.1 = (bf16[2,3,4,128]{3,2,1,0:T(4,128)(2,1)S(1)}, bf16[2,3,4,128]{3,2,1,0:T(4,128)(2,1)}, u32[]{:S(2)}) copy-start(bf16[2,3,4,128]{3,2,1,0:T(4,128)(2,1)} %param.7) | copy-start | bytes 18436
where the time goes:
time: 30.4 us; the launch traced here: 30 us
  blocking collectives  23.9 us (79%)
  local copies, waits for them, and re-layouts  4.13 us (14%)
  matrix products  1.53 us (5%)
  other arithmetic  0.37 us (1%)
    all_gather x1, blocking collectives, on_device(): all_planes = lax.all_gather(cube, 'bm', axis=2, tiled=True)  13.3 us
    all_gather x1, blocking collectives, on_device(): lax.all_gather(sky_alm, 'det', axis=2, tiled=True)  10.6 us
    unnamed x9, local copies, waits for them, and re-layouts  1.81 us
    dot_general x4, matrix products, product_first(): lax.dot_general(left, right, dims, precision=lax.Precision.HIGHEST, prefe...  1.3 us
    dynamic_slice x2, local copies, waits for them, and re-layouts, columns(): return lax.dynamic_slice_in_dim(values, offset, width, 1).reshape(-1)  0.89 us
    reshape x1, local copies, waits for them, and re-layouts, on_device(): return result.reshape(theta_index.shape[0], width)  0.67 us

commit v1 on v0

v1 whole, which is shorter than its diff:
```python
import functools
import math

import jax
import jax.numpy as jnp
from jax import lax
from jax.experimental import pallas as pl
from jax.experimental.pallas import tpu as pltpu
from jax.sharding import PartitionSpec as P

NPHI = 16384
NPSI = 32
LANES = 128
SUBLANES = 8

SIN_TERMS = (1.0, -1 / 6, 1 / 120, -1 / 5040, 1 / 362880)
COS_TERMS = (1.0, -1 / 2, 1 / 24, -1 / 720, 1 / 40320)


def kernel_call(body, outs, *args, scalars=1, flops=0):
    spaces = [pltpu.SMEM] * scalars + [pltpu.VMEM] * (len(args) - scalars)
    return pl.pallas_call(
        body,
        out_shape=outs,
        in_specs=[pl.BlockSpec(memory_space=space) for space in spaces],
        out_specs=jax.tree.map(lambda _: pl.BlockSpec(memory_space=pltpu.VMEM), outs),
        cost_estimate=pl.CostEstimate(flops=flops, bytes_accessed=0, transcendentals=0),
        compiler_params=pltpu.CompilerParams(vmem_limit_bytes=16 << 20),
    )(*args)


def cos_sin(steps, period):
    quarter = steps.astype(jnp.float32) * (4.0 / period)
    nearest = jnp.floor(quarter + 0.5)
    angle = (quarter - nearest) * (math.pi / 2)
    square = angle * angle
    sine, cosine = SIN_TERMS[-1], COS_TERMS[-1]
    for s_term, c_term in zip(SIN_TERMS[-2::-1], COS_TERMS[-2::-1]):
        sine, cosine = sine * square + s_term, cosine * square + c_term
    sine = sine * angle
    turn = nearest.astype(jnp.int32)
    swap, low = (turn & 1) == 1, (turn & 2) == 2
    c_abs, s_abs = jnp.where(swap, sine, cosine), jnp.where(swap, cosine, sine)
    return jnp.where(swap != low, -c_abs, c_abs), jnp.where(low, -s_abs, s_abs)


def features(cycles, planes, own_ref, theta_ref, phi_ref, psi_ref, cos_ref, sin_ref, first_ref, second_ref):
    own = own_ref[0]
    modes = cos_ref.shape[0]
    halves = first_ref.shape[0]
    wide = 2 * planes
    for row in range(theta_ref.shape[0]):
        at = pl.ds(row * LANES, LANES)
        theta, phi, psi = (ref[row : row + 1, :] for ref in (theta_ref, phi_ref, psi_ref))
        step = min(modes, 2 * SUBLANES)

        def turn_phi(first, at=at, phi=phi, step=step):
            mode = first + lax.broadcasted_iota(jnp.int32, (step, LANES), 0)
            c, s = cos_sin((mode * phi) & (NPHI - 1), NPHI)
            cos_ref[pl.ds(first, step), at] = c
            sin_ref[pl.ds(first, step), at] = s

        if modes == step:
            turn_phi(0)
        else:
            pl.loop(0, modes, step=step)(turn_phi)
        for half in range(halves):
            inner = lax.broadcasted_iota(jnp.int32, (wide, LANES), 0)
            part = (own ^ (2 * half)) ^ (inner // planes)
            plane = part * planes + inner % planes
            c, s = cos_sin((plane * psi) & (NPSI - 1), NPSI)
            chosen = [theta == cycle for cycle in range(cycles)]
            cs = [jnp.where(pick, c, 0.0) for pick in chosen]
            ss = [jnp.where(pick, s, 0.0) for pick in chosen]
            for ref, rows in ((first_ref, cs + [-v for v in ss]), (second_ref, ss + cs)):
                full = jnp.concatenate(rows, axis=0)
                high = full.astype(jnp.bfloat16)
                low = (full - high.astype(jnp.float32)).astype(jnp.bfloat16)
                ref[half, :, at] = jnp.concatenate([high, high, low, jnp.zeros_like(low)], axis=0)


def cubes(masks, place_ref, near_ref, far_ref, beam_ref, beam_far_ref, table_ref, table_far_ref, out_ref):
    place = place_ref[0]
    cycles, modes, planes, band = table_ref.shape
    blocks = near_ref.shape[0]
    each = near_ref.shape[3]
    f32 = jnp.float32
    beam = [
        [jnp.concatenate([beam_ref[k, c], beam_far_ref[k, c]], axis=0).astype(f32) for c in range(beam_ref.shape[1])]
        for k in range(2)
    ]
    rows = 2 * cycles * 2 * planes

    def one_mode(mode, block, inner, total):
        sky = [
            [
                jnp.where(
                    block < blocks,
                    near_ref[block & (blocks - 1), k, c, inner : inner + 1, :],
                    far_ref[block & (blocks - 1), k, c, inner : inner + 1, :],
                ).astype(f32)
                for c in range(near_ref.shape[2])
            ]
            for k in range(2)
        ]
        real = sum(sky[0][c] * beam[0][c] - sky[1][c] * beam[1][c] for c in range(len(beam[0])))
        imag = sum(sky[0][c] * beam[1][c] + sky[1][c] * beam[0][c] for c in range(len(beam[0])))
        spectra = [v.astype(jnp.bfloat16).astype(f32) for v in (real, imag)]
        tables = [
            jnp.concatenate([table_ref[g, mode], table_far_ref[g, mode]], axis=0).astype(f32) for g in range(cycles)
        ]
        products = jnp.concatenate([s * t for s in spectra for t in tables], axis=0)
        sums = jnp.sum(products, axis=1, keepdims=True)
        lane = lax.broadcasted_iota(jnp.int32, (rows, LANES), 1)
        return jnp.where(lane == mode % LANES, sums, total)

    def block_of(owner):
        rest, block = owner ^ place, 0
        for level, mask in enumerate(masks):
            bit = (rest >> (mask.bit_length() - 1)) & 1
            rest = rest ^ (bit * mask)
            block = block | (bit << level)
        return block

    for base in range(0, modes, LANES):
        count = min(modes, LANES)
        total = jnp.zeros((rows, LANES), f32)
        if count * cycles <= LANES:
            for mode in range(base, base + count):
                total = one_mode(mode, block_of(mode // each), mode % each, total)
        else:

            def owned(owner, total):
                for inner in range(each):
                    total = one_mode(owner * each + inner, block_of(owner), inner, total)
                return total

            total = lax.fori_loop(base // each, (base + count) // each, owned, total)
        out_ref[base : base + count, :] = jnp.concatenate([total, total], axis=0).T[:count]


def sampled(cube, cos_ref, sin_ref, first, second, row):
    rows = cube.shape[1] // 2
    at = pl.ds(row * LANES, LANES)
    high = cube.astype(jnp.bfloat16)
    low = (cube - high.astype(jnp.float32)).astype(jnp.bfloat16)
    lane = lax.broadcasted_iota(jnp.int32, cube.shape, 1)
    left = jnp.concatenate([jnp.where(lane < rows, high, low), high], axis=1)
    real = jnp.dot(left, first[:, at], preferred_element_type=jnp.float32)
    imag = jnp.dot(left, second[:, at], preferred_element_type=jnp.float32)
    return jnp.sum(real * cos_ref[:, at] - imag * sin_ref[:, at], axis=0, keepdims=True)


def near_half(cube_ref, cos_ref, sin_ref, first_ref, second_ref, out_ref):
    cube = cube_ref[...]
    for row in range(out_ref.shape[0]):
        out_ref[row : row + 1, :] = sampled(cube, cos_ref, sin_ref, first_ref.at[0], second_ref.at[0], row)


def far_half(start, cube_ref, cos_ref, sin_ref, first_ref, second_ref, near_ref, out_ref):
    rows, width = near_ref.shape[0], out_ref.shape[1]
    done = []
    for row in range(rows):
        total = near_ref[row : row + 1, :]
        for half in range(cube_ref.shape[0]):
            total += sampled(
                cube_ref[half], cos_ref, sin_ref, first_ref.at[start + half], second_ref.at[start + half], row
            )
        done.append(total)
    whole = jnp.concatenate(done, axis=0)
    for part in range(LANES // width):
        out_ref[part * rows : (part + 1) * rows, :] = whole[:, part * width : (part + 1) * width]


def on_device(sky_alm, beam_blm, wigner, theta_index, phi_index, psi_index):
    f32, bf16 = jnp.float32, jnp.bfloat16
    groups, parts = lax.axis_size("det"), lax.axis_size("bm")
    place, own = lax.axis_index("det"), lax.axis_index("bm")
    cycles, modes, planes, _ = wigner.shape
    detectors = theta_index.shape[0]
    width = theta_index.shape[1] // parts
    packed = LANES // width
    samples = detectors * width

    def trade(values, axis, mask):
        return lax.ppermute(values, axis, [(i, i ^ mask) for i in range(lax.axis_size(axis))])

    masks = [(1 << level) | 1 for level in reversed(range(1, groups.bit_length() - 1))] + [1]
    near = sky_alm[None]
    far = trade(near, "det", masks[0])
    table_far = trade(wigner, "bm", 1)
    beam_far = trade(beam_blm, "bm", 1)
    for mask in masks[1:]:
        near = jnp.concatenate([near, far])
        far = trade(near, "det", mask)

    def columns(values):
        held = lax.dynamic_slice_in_dim(values, own * width, width, 1)
        return held.reshape(packed, detectors // packed, width).swapaxes(0, 1).reshape(-1, LANES)

    rows = 2 * cycles * 2 * planes
    factors = jax.ShapeDtypeStruct((parts // 2, 4 * rows, samples), bf16)
    waves = jax.ShapeDtypeStruct((modes, samples), f32)
    cosine, sine, first, second = kernel_call(
        functools.partial(features, cycles, planes),
        [waves, waves, factors, factors],
        own.reshape(1),
        columns(theta_index),
        columns(phi_index),
        columns(psi_index),
    )
    half = kernel_call(
        functools.partial(cubes, masks),
        jax.ShapeDtypeStruct((modes, 2 * rows), f32),
        place.reshape(1),
        near,
        far,
        beam_blm,
        beam_far,
        wigner,
        table_far,
    )
    held, others, bit = half[None], [], 2
    while bit < parts:
        others.append(trade(held, "bm", bit))
        if 2 * bit < parts:
            held = jnp.concatenate([held, others[-1]])
        bit *= 2
    partial = kernel_call(
        near_half, jax.ShapeDtypeStruct((samples // LANES, LANES), f32), half, cosine, sine, first, second, scalars=0
    )
    others = others[0] if len(others) == 1 else jnp.concatenate(others)
    return kernel_call(
        functools.partial(far_half, 1),
        jax.ShapeDtypeStruct((detectors, width), f32),
        others,
        cosine,
        sine,
        first,
        second,
        partial,
        scalars=0,
    )


def solution(mesh):
    placed = (
        P(None, None, "det", None),
        P(None, None, "bm", None),
        P("det", None, "bm", None),
        P("det", None),
        P("det", None),
        P("det", None),
    )
    return jax.shard_map(
        on_device, mesh=mesh, in_specs=placed, out_specs=P("det", "bm"), check_vma=False
    )
```

time: 30.4 us -> 18.8 us (0.62)
  blocking collectives: 23.9 us -> 0 us
  starting transfers between devices: 0 us -> 9.17 us
  waiting for transfers between devices: 0 us -> 4.7 us
  local copies, waits for them, and re-layouts: 4.13 us -> 1.14 us
  Pallas kernels: 0 us -> 2.12 us
  matrix products: 1.53 us -> 0 us
  other arithmetic: 0.37 us -> 1.4 us
    all_gather x2 -> x0, blocking collectives: 23.9 us -> none  [the longest x1 13.3 us: on_device(): all_planes = lax.all_gather(cube, 'bm', axis=2, tiled=True)]
    ppermute x0 -> x6, starting transfers between devices: none -> 9.17 us  [trade(): lax.ppermute(values, axis, [(i, i ^ mask) for i in range(lax.axis_size(ax...]
    ppermute x0 -> x6, waiting for transfers between devices: none -> 4.7 us  [trade(): lax.ppermute(values, axis, [(i, i ^ mask) for i in range(lax.axis_size(ax...]
    pallas_call x0 -> x4, Pallas kernels: none -> 2.12 us  [kernel_call(): pl.pallas_call(body, out_shape=outs, in_specs=[pl.BlockSpec(memory_space=...]
    unnamed x9 -> x6, local copies, waits for them, and re-layouts: 1.81 us -> 0.01 us
    dot_general x5 -> x0, matrix products: 1.53 us -> none  [the longest x4 1.3 us: product_first(): lax.dot_general(left, right, dims, precision=lax.Precision.HIGHEST, prefe...]
    concatenate x0 -> x2, other arithmetic: none -> 1.4 us  [on_device(): near = jnp.concatenate([near, far])]
    dynamic_slice x2 -> x0, local copies, waits for them, and re-layouts: 0.89 us -> none  [columns(): return lax.dynamic_slice_in_dim(values, offset, width, 1).reshape(-1)]
  transfers between devices with their start and end apart: 0 -> 6, of which waited for: 0 -> 5; matrix products, arithmetic and copies ran while one was open for 0% -> 10% of each run, Pallas kernels for 0% -> 5%
where the time goes in v1:
time: 18.8 us; the launch traced here: 18.6 us
  starting transfers between devices  9.17 us (49%)
  waiting for transfers between devices  4.7 us (25%)
  Pallas kernels  2.12 us (11%)
  other arithmetic  1.4 us (7%)
  local copies, waits for them, and re-layouts  1.14 us (6%)
    ppermute x6, starting transfers between devices, trade(): lax.ppermute(values, axis, [(i, i ^ mask) for i in range(lax.axis_size(ax...  9.17 us
    ppermute x6, waiting for transfers between devices, trade(): lax.ppermute(values, axis, [(i, i ^ mask) for i in range(lax.axis_size(ax...  4.7 us
    pallas_call x4, Pallas kernels, kernel_call(): pl.pallas_call(body, out_shape=outs, in_specs=[pl.BlockSpec(memory_space=...  2.12 us
    concatenate x2, other arithmetic, on_device(): near = jnp.concatenate([near, far])  1.4 us
    transpose x5, local copies, waits for them, and re-layouts, columns(): held.reshape(packed, detectors // packed, width).swapaxes(0, 1)  0.88 us
  transfers between devices with their start and end apart: 6, of which 5 were waited for; matrix products, arithmetic and copies ran while one was open for 10% of the time, Pallas kernels for 5%

profile of v1, /device:TPU:0, one launch (start us, length us, event | category | flops | bytes accessed | tf_op | source)
XLA Modules:
  0.0 18.6 jit_solution(2036017570270859579)
XLA Ops:
  0.0 0.0 copy-start
  0.0 0.0 copy-start.1
  0.0 2.4 %collective-permute-start = (bf16[1,2,3,2,128]{4,3,2,1,0:T(2,128)(2,1)}, bf16[1,2,3,2,128]{4,3,2,1,0:T(2,128)(2,1)S(1)}, u32[]{:S(2)}, u32[]{:S(2)}) collective-permute-start(bf16[1,2,3,2,128]{4,3,2,1,0:T(2,128)(2,1)} %bitcast.17), channel_id=1, source_target_pairs={{0,20},{4,16},{8,28},{12,24},{16,4},{20,0},{24,12},{28,8},{1,21},{... | collective-permute-start | bytes 9224 | tf_op jit(solution)/shard_map/ppermute | solution.py:186
  2.4 1.5 %collective-permute-done = bf16[1,2,3,2,128]{4,3,2,1,0:T(2,128)(2,1)S(1)} collective-permute-done((bf16[1,2,3,2,128]{4,3,2,1,0:T(2,128)(2,1)}, bf16[1,2,3,2,128]{4,3,2,1,0:T(2,128)(2,1)S(1)}, u32[]{:S(2)}, u32[]{:S(2)}) %collective-permute-start) | collective-permute-done | bytes 3104 | tf_op jit(solution)/shard_map/ppermute | solution.py:186
  4.0 0.7 %pad_maximum_fusion.1 = bf16[2,2,3,2,128]{4,3,2,1,0:T(2,128)(2,1)S(1)} fusion(bf16[1,2,3,2,128]{4,3,2,1,0:T(2,128)(2,1)S(1)} %collective-permute-done, bf16[1,2,3,2,128]{4,3,2,1,0:T(2,128)(2,1)} %bitcast.18), kind=kLoop, calls=%fused_computation.4 | loop fusion | flops 3072 | bytes 12288 | tf_op jit(solution)/shard_map/concatenate | solution.py:194
  4.7 2.0 %collective-permute-start.1 = (bf16[2,2,3,2,128]{4,3,2,1,0:T(2,128)(2,1)S(1)}, bf16[2,2,3,2,128]{4,3,2,1,0:T(2,128)(2,1)S(1)}, u32[]{:S(2)}, u32[]{:S(2)}) collective-permute-start(bf16[2,2,3,2,128]{4,3,2,1,0:T(2,128)(2,1)S(1)} %pad_maximum_fusion.1), channel_id=1, source_target_pairs={{0,12},{4,8},{8,4},{12,0},{16,28},{20,24},{24,20},{28,16},{1,13},{... | collective-permute-start | bytes 18440 | tf_op jit(solution)/shard_map/ppermute | solution.py:186
  6.7 1.6 %collective-permute-start.3 = (bf16[2,3,4,128]{3,2,1,0:T(4,128)(2,1)}, bf16[2,3,4,128]{3,2,1,0:T(4,128)(2,1)S(1)}, u32[]{:S(2)}, u32[]{:S(2)}) collective-permute-start(bf16[2,3,4,128]{3,2,1,0:T(4,128)(2,1)} %beam_ref.1), channel_id=1, source_target_pairs={{0,1},{1,0},{2,3},{3,2},{4,5},{5,4},{6,7},{7,6},{8,9},{9,8},{10,11... | collective-permute-start | bytes 18440 | tf_op jit(solution)/shard_map/ppermute | solution.py:186
  8.3 0.4 %collective-permute-start.4 = (bf16[4,16,4,128]{3,2,1,0:T(4,128)(2,1)}, bf16[4,16,4,128]{3,2,1,0:T(4,128)(2,1)S(1)}, u32[]{:S(2)}, u32[]{:S(2)}) collective-permute-start(bf16[4,16,4,128]{3,2,1,0:T(4,128)(2,1)} %table_ref.1), channel_id=1, source_target_pairs={{0,1},{1,0},{2,3},{3,2},{4,5},{5,4},{6,7},{7,6},{8,9},{9,8},{10,11... | collective-permute-start | bytes 196616 | tf_op jit(solution)/shard_map/ppermute | solution.py:186
  8.7 0.0 collective-permute-done.1
  8.7 0.7 %pad_maximum_fusion.near_ref = bf16[4,2,3,2,128]{4,3,2,1,0:T(2,128)(2,1)S(1)} fusion(bf16[2,2,3,2,128]{4,3,2,1,0:T(2,128)(2,1)S(1)} %collective-permute-done.1, bf16[1,2,3,2,128]{4,3,2,1,0:T(2,128)(2,1)S(1)} %collective-permute-done, bf16[1,2,3,2,128]{4,3,2,1,0:T(2,128)(2,1)} %bitcast.19), kind=kLoop, calls=%fused_computation | loop fusion | flops 12288 | bytes 24576 | tf_op jit(solution)/shard_map/concatenate | solution.py:194
  9.4 0.1 collective-permute-start.2
  9.5 0.8 %dynamic-slice_bitcast_fusion = (s32[8,2,64]{2,0,1:T(8,128)S(1)}, s32[8,2,64]{2,0,1:T(8,128)S(1)}) fusion(s32[16,256]{1,0:T(8,128)} %param.11, s32[]{:T(128)S(6)} %select_n.2, s32[16,256]{1,0:T(8,128)} %param.10), kind=kLoop, calls=%fused_computation.1 | loop fusion | bytes 16388 | tf_op jit(solution)/shard_map/transpose | solution.py:199
  10.3 0.0 copy-start.2
  10.3 0.2 %collective-permute-done.3.beam_far_ref = bf16[2,3,4,128]{3,2,1,0:T(4,128)(2,1)S(1)} collective-permute-done((bf16[2,3,4,128]{3,2,1,0:T(4,128)(2,1)}, bf16[2,3,4,128]{3,2,1,0:T(4,128)(2,1)S(1)}, u32[]{:S(2)}, u32[]{:S(2)}) %collective-permute-start.3) | collective-permute-done | bytes 6176 | tf_op jit(solution)/shard_map/ppermute | solution.py:186
  10.5 0.1 collective-permute-done.2.far_ref
  10.7 2.1 %collective-permute-done.4.table_far_ref = bf16[4,16,4,128]{3,2,1,0:T(4,128)(2,1)S(1)} collective-permute-done((bf16[4,16,4,128]{3,2,1,0:T(4,128)(2,1)}, bf16[4,16,4,128]{3,2,1,0:T(4,128)(2,1)S(1)}, u32[]{:S(2)}, u32[]{:S(2)}) %collective-permute-start.4) | collective-permute-done | bytes 65568 | tf_op jit(solution)/shard_map/ppermute | solution.py:186
  12.7 0.0 copy-done.1
  12.7 0.0 copy-done.2
  12.7 0.3 %shard_map.64.cube_ref = f32[16,128]{1,0:T(8,128)S(1)} custom-call(s32[1]{0:T(128)} %bitcast.place_ref, bf16[4,2,3,2,128]{4,3,2,1,0:T(2,128)(2,1)S(1)} %pad_maximum_fusion.near_ref, bf16[4,2,3,2,128]{4,3,2,1,0:T(2,128)(2,1)S(1)} %collective-permute-done.2.far_ref, bf16[2,3,4,128]{3,2,1,0:T(4,128)(2,1)S(1)} %copy-done.2, ...), custom_call_target="tpu_custom_call" | custom-call | tf_op jit(solution)/shard_map/pallas_call | solution.py:22
  13.0 2.6 %collective-permute-start.5 = (f32[1,16,128]{2,1,0:T(8,128)S(1)}, f32[1,16,128]{2,1,0:T(8,128)S(1)}, u32[]{:S(2)}, u32[]{:S(2)}) collective-permute-start(f32[1,16,128]{2,1,0:T(8,128)S(1)} %bitcast.16), channel_id=1, source_target_pairs={{0,2},{1,3},{2,0},{3,1},{4,6},{5,7},{6,4},{7,5},{8,10},{9,11},{10,... | collective-permute-start | bytes 24584 | tf_op jit(solution)/shard_map/ppermute | solution.py:186
  15.7 0.0 copy-done
  15.7 0.1 dynamic-slice_bitcast_fusion.2
  15.7 0.1 reshape.27.theta_ref
  15.8 0.1 reshape.31.psi_ref
  15.9 0.1 reshape.29.phi_ref
  16.0 0.6 %shard_map.65 = (f32[16,1024]{1,0:T(8,128)S(1)}, f32[16,1024]{1,0:T(8,128)S(1)}, bf16[2,256,1024]{2,1,0:T(8,128)(2,1)S(1)}, bf16[2,256,1024]{2,1,0:T(8,128)(2,1)S(1)}) custom-call(s32[1]{0:T(128)} %bitcast.3.own_ref, s32[8,128]{1,0:T(8,128)S(1)} %reshape.27.theta_ref, s32[8,128]{1,0:T(8,128)S(1)} %reshape.29.phi_ref, s32[8,128]{1,0:T(8,128)S(1)} %reshape.31.psi_ref), custom_call_target="tpu_custom_call" | custom-call | tf_op jit(solution)/shard_map/pallas_call | solution.py:22
  16.6 0.3 %shard_map.66.near_ref = f32[8,128]{1,0:T(8,128)S(1)} custom-call(f32[16,128]{1,0:T(8,128)S(1)} %shard_map.64.cube_ref, f32[16,1024]{1,0:T(8,128)S(1)} %get-tuple-element.9.cos_ref, f32[16,1024]{1,0:T(8,128)S(1)} %get-tuple-element.10.sin_ref, bf16[2,256,1024]{2,1,0:T(8,128)(2,1)S(1)} %get-tuple-element.11.first_ref, ...), custom_call_target="tpu_custom_call" | custom-call | tf_op jit(solution)/shard_map/pallas_call | solution.py:22
  16.9 0.7 %collective-permute-done.5.cube_ref = f32[1,16,128]{2,1,0:T(8,128)S(1)} collective-permute-done((f32[1,16,128]{2,1,0:T(8,128)S(1)}, f32[1,16,128]{2,1,0:T(8,128)S(1)}, u32[]{:S(2)}, u32[]{:S(2)}) %collective-permute-start.5) | collective-permute-done | bytes 8224 | tf_op jit(solution)/shard_map/ppermute | solution.py:186
  17.6 1.0 %shard_map.67 = f32[16,64]{1,0:T(8,128)} custom-call(f32[1,16,128]{2,1,0:T(8,128)S(1)} %collective-permute-done.5.cube_ref, f32[16,1024]{1,0:T(8,128)S(1)} %get-tuple-element.9.cos_ref, f32[16,1024]{1,0:T(8,128)S(1)} %get-tuple-element.10.sin_ref, bf16[2,256,1024]{2,1,0:T(8,128)(2,1)S(1)} %get-tuple-element.11.first_ref, ...), custom_call_target="tpu_custom_call" | custom-call | tf_op jit(solution)/shard_map/pallas_call | solution.py:22
  (3 shorter events, 0.0 us)
Async XLA Ops:
  0.0 15.7 %copy-start = (s32[16,256]{1,0:T(8,128)S(1)}, s32[16,256]{1,0:T(8,128)}, u32[]{:S(2)}) copy-start(s32[16,256]{1,0:T(8,128)} %param.9) | copy-start | bytes 49156
  0.0 12.7 %copy-start.1 = (bf16[4,16,4,128]{3,2,1,0:T(4,128)(2,1)S(1)}, bf16[4,16,4,128]{3,2,1,0:T(4,128)(2,1)}, u32[]{:S(2)}) copy-start(bf16[4,16,4,128]{3,2,1,0:T(4,128)(2,1)} %table_ref.1) | copy-start | bytes 196612
  0.0 4.0 %collective-permute-start = (bf16[1,2,3,2,128]{4,3,2,1,0:T(2,128)(2,1)}, bf16[1,2,3,2,128]{4,3,2,1,0:T(2,128)(2,1)S(1)}, u32[]{:S(2)}, u32[]{:S(2)}) collective-permute-start(bf16[1,2,3,2,128]{4,3,2,1,0:T(2,128)(2,1)} %bitcast.17), channel_id=1, source_target_pairs={{0,20},{4,16},{8,28},{12,24},{16,4},{20,0},{24,12},{28,8},{1,21},{... | collective-permute-start | bytes 9224 | tf_op jit(solution)/shard_map/ppermute | solution.py:186
  4.7 4.1 %collective-permute-start.1 = (bf16[2,2,3,2,128]{4,3,2,1,0:T(2,128)(2,1)S(1)}, bf16[2,2,3,2,128]{4,3,2,1,0:T(2,128)(2,1)S(1)}, u32[]{:S(2)}, u32[]{:S(2)}) collective-permute-start(bf16[2,2,3,2,128]{4,3,2,1,0:T(2,128)(2,1)S(1)} %pad_maximum_fusion.1), channel_id=1, source_target_pairs={{0,12},{4,8},{8,4},{12,0},{16,28},{20,24},{24,20},{28,16},{1,13},{... | collective-permute-start | bytes 18440 | tf_op jit(solution)/shard_map/ppermute | solution.py:186
  6.7 3.8 %collective-permute-start.3 = (bf16[2,3,4,128]{3,2,1,0:T(4,128)(2,1)}, bf16[2,3,4,128]{3,2,1,0:T(4,128)(2,1)S(1)}, u32[]{:S(2)}, u32[]{:S(2)}) collective-permute-start(bf16[2,3,4,128]{3,2,1,0:T(4,128)(2,1)} %beam_ref.1), channel_id=1, source_target_pairs={{0,1},{1,0},{2,3},{3,2},{4,5},{5,4},{6,7},{7,6},{8,9},{9,8},{10,11... | collective-permute-start | bytes 18440 | tf_op jit(solution)/shard_map/ppermute | solution.py:186
  8.3 4.5 %collective-permute-start.4 = (bf16[4,16,4,128]{3,2,1,0:T(4,128)(2,1)}, bf16[4,16,4,128]{3,2,1,0:T(4,128)(2,1)S(1)}, u32[]{:S(2)}, u32[]{:S(2)}) collective-permute-start(bf16[4,16,4,128]{3,2,1,0:T(4,128)(2,1)} %table_ref.1), channel_id=1, source_target_pairs={{0,1},{1,0},{2,3},{3,2},{4,5},{5,4},{6,7},{7,6},{8,9},{9,8},{10,11... | collective-permute-start | bytes 196616 | tf_op jit(solution)/shard_map/ppermute | solution.py:186
  9.4 1.2 %collective-permute-start.2 = (bf16[4,2,3,2,128]{4,3,2,1,0:T(2,128)(2,1)S(1)}, bf16[4,2,3,2,128]{4,3,2,1,0:T(2,128)(2,1)S(1)}, u32[]{:S(2)}, u32[]{:S(2)}) collective-permute-start(bf16[4,2,3,2,128]{4,3,2,1,0:T(2,128)(2,1)S(1)} %pad_maximum_fusion.near_ref), channel_id=1, source_target_pairs={{0,4},{4,0},{8,12},{12,8},{16,20},{20,16},{24,28},{28,24},{1,5},{5... | collective-permute-start | bytes 36872 | tf_op jit(solution)/shard_map/ppermute | solution.py:186
  10.3 2.4 %copy-start.2 = (bf16[2,3,4,128]{3,2,1,0:T(4,128)(2,1)S(1)}, bf16[2,3,4,128]{3,2,1,0:T(4,128)(2,1)}, u32[]{:S(2)}) copy-start(bf16[2,3,4,128]{3,2,1,0:T(4,128)(2,1)} %beam_ref.1) | copy-start | bytes 18436
  13.0 4.6 %collective-permute-start.5 = (f32[1,16,128]{2,1,0:T(8,128)S(1)}, f32[1,16,128]{2,1,0:T(8,128)S(1)}, u32[]{:S(2)}, u32[]{:S(2)}) collective-permute-start(f32[1,16,128]{2,1,0:T(8,128)S(1)} %bitcast.16), channel_id=1, source_target_pairs={{0,2},{1,3},{2,0},{3,1},{4,6},{5,7},{6,4},{7,5},{8,10},{9,11},{10,... | collective-permute-start | bytes 24584 | tf_op jit(solution)/shard_map/ppermute | solution.py:186

commit v2 on v1

--- a/solution.py
+++ b/solution.py
@@ -7,6 +7,7 @@
 from jax.experimental import pallas as pl
 from jax.experimental.pallas import tpu as pltpu
 from jax.sharding import PartitionSpec as P
+
 
 NPHI = 16384
 NPSI = 32
@@ -27,6 +28,19 @@
         cost_estimate=pl.CostEstimate(flops=flops, bytes_accessed=0, transcendentals=0),
         compiler_params=pltpu.CompilerParams(vmem_limit_bytes=16 << 20),
     )(*args)
+
+
+def staged(sky_ref, beam_ref, table_ref, sky_out, pack_out, sems):
+    rows = table_ref.shape[0]
+    copies = [
+        pltpu.make_async_copy(sky_ref, sky_out, sems.at[0]),
+        pltpu.make_async_copy(table_ref, pack_out.at[:rows], sems.at[1]),
+        pltpu.make_async_copy(beam_ref, pack_out.at[rows:], sems.at[2]),
+    ]
+    for copy in copies:
+        copy.start()
+    for copy in copies:
+        copy.wait()
 
 
 def cos_sin(steps, period):
@@ -79,16 +93,17 @@
                 ref[half, :, at] = jnp.concatenate([high, high, low, jnp.zeros_like(low)], axis=0)
 
 
-def cubes(masks, place_ref, near_ref, far_ref, beam_ref, beam_far_ref, table_ref, table_far_ref, out_ref):
+def cubes(masks, cycles, place_ref, near_ref, far_ref, pack_ref, pack_far_ref, out_ref):
     place = place_ref[0]
-    cycles, modes, planes, band = table_ref.shape
-    blocks = near_ref.shape[0]
-    each = near_ref.shape[3]
+    modes = out_ref.shape[0]
+    planes = pack_ref.shape[1]
+    blocks, kinds, each = near_ref.shape[0], near_ref.shape[2], near_ref.shape[3]
     f32 = jnp.float32
-    beam = [
-        [jnp.concatenate([beam_ref[k, c], beam_far_ref[k, c]], axis=0).astype(f32) for c in range(beam_ref.shape[1])]
-        for k in range(2)
-    ]
+
+    def both(row):
+        return jnp.concatenate([pack_ref[row], pack_far_ref[row]], axis=0).astype(f32)
+
+    beam = [[both(cycles * modes + k * kinds + c) for c in range(kinds)] for k in range(2)]
     rows = 2 * cycles * 2 * planes
 
     def one_mode(mode, block, inner, total):
@@ -99,16 +114,14 @@
                     near_ref[block & (blocks - 1), k, c, inner : inner + 1, :],
                     far_ref[block & (blocks - 1), k, c, inner : inner + 1, :],
                 ).astype(f32)
-                for c in range(near_ref.shape[2])
+                for c in range(kinds)
             ]
             for k in range(2)
         ]
-        real = sum(sky[0][c] * beam[0][c] - sky[1][c] * beam[1][c] for c in range(len(beam[0])))
-        imag = sum(sky[0][c] * beam[1][c] + sky[1][c] * beam[0][c] for c in range(len(beam[0])))
+        real = sum(sky[0][c] * beam[0][c] - sky[1][c] * beam[1][c] for c in range(kinds))
+        imag = sum(sky[0][c] * beam[1][c] + sky[1][c] * beam[0][c] for c in range(kinds))
         spectra = [v.astype(jnp.bfloat16).astype(f32) for v in (real, imag)]
-        tables = [
-            jnp.concatenate([table_ref[g, mode], table_far_ref[g, mode]], axis=0).astype(f32) for g in range(cycles)
-        ]
+        tables = [both(g * modes + mode) for g in range(cycles)]
         products = jnp.concatenate([s * t for s in spectra for t in tables], axis=0)
         sums = jnp.sum(products, axis=1, keepdims=True)
         lane = lax.broadcasted_iota(jnp.int32, (rows, LANES), 1)
@@ -182,14 +195,31 @@
     packed = LANES // width
     samples = detectors * width
 
+    def in_hbm(values):
+        return pltpu.with_memory_space_constraint(values, pltpu.HBM)
+
     def trade(values, axis, mask):
         return lax.ppermute(values, axis, [(i, i ^ mask) for i in range(lax.axis_size(axis))])
 
+    sky, pack = pl.pallas_call(
+        staged,
+        out_shape=[
+            jax.ShapeDtypeStruct((1,) + sky_alm.shape, bf16),
+            jax.ShapeDtypeStruct((cycles * modes + 2 * beam_blm.shape[1],) + wigner.shape[2:], bf16),
+        ],
+        in_specs=[pl.BlockSpec(memory_space=pltpu.HBM)] * 3,
+        out_specs=[pl.BlockSpec(memory_space=pltpu.VMEM)] * 2,
+        scratch_shapes=[pltpu.SemaphoreType.DMA((3,))],
+        compiler_params=pltpu.CompilerParams(vmem_limit_bytes=16 << 20),
+    )(
+        in_hbm(sky_alm[None]),
+        in_hbm(beam_blm.reshape((-1,) + beam_blm.shape[2:])),
+        in_hbm(wigner.reshape((-1,) + wigner.shape[2:])),
+    )
     masks = [(1 << level) | 1 for level in reversed(range(1, groups.bit_length() - 1))] + [1]
-    near = sky_alm[None]
+    near = sky
     far = trade(near, "det", masks[0])
-    table_far = trade(wigner, "bm", 1)
-    beam_far = trade(beam_blm, "bm", 1)
+    pack_far = trade(pack, "bm", 1)
     for mask in masks[1:]:
         near = jnp.concatenate([near, far])
         far = trade(near, "det", mask)
@@ -210,15 +240,13 @@
         columns(psi_index),
     )
     half = kernel_call(
-        functools.partial(cubes, masks),
+        functools.partial(cubes, masks, cycles),
         jax.ShapeDtypeStruct((modes, 2 * rows), f32),
         place.reshape(1),
         near,
         far,
-        beam_blm,
-        beam_far,
-        wigner,
-        table_far,
+        pack,
+        pack_far,
     )
     held, others, bit = half[None], [], 2
     while bit < parts:

time: 18.8 us -> 15.5 us (0.82)
  waiting for transfers between devices: 4.7 us -> 2.54 us
  other arithmetic: 1.4 us -> 0.01 us
  Pallas kernels: 2.12 us -> 3.01 us
  local copies, waits for them, and re-layouts: 1.14 us -> 0.45 us
    ppermute x6 -> x5, waiting for transfers between devices: 4.7 us -> 2.54 us  [trade(): lax.ppermute(values, axis, [(i, i ^ mask) for i in range(lax.axis_size(ax...]
    concatenate x2 -> x1, other arithmetic: 1.4 us -> 0.01 us  [on_device(): near = jnp.concatenate([near, far])]
    pallas_call x0 -> x1, Pallas kernels: none -> 0.89 us  [on_device(): pl.pallas_call(staged, out_shape=[jax.ShapeDtypeStruct((1,) + sky_alm.sha...]
    transpose x5, local copies, waits for them, and re-layouts: 0.88 us -> 0.16 us  [columns(): held.reshape(packed, detectors // packed, width).swapaxes(0, 1)]
    ppermute x6 -> x5, starting transfers between devices: 9.17 us -> 9.29 us  [trade(): lax.ppermute(values, axis, [(i, i ^ mask) for i in range(lax.axis_size(ax...]
  transfers between devices with their start and end apart: 6 -> 5, of which waited for: 5 -> 3; matrix products, arithmetic and copies ran while one was open for 10% -> 3% of each run, Pallas kernels for 5% -> 6%
where the time goes in v2:
time: 15.5 us; the launch traced here: 15.4 us
  starting transfers between devices  9.29 us (60%)
  Pallas kernels  3.01 us (19%)
  waiting for transfers between devices  2.54 us (16%)
  local copies, waits for them, and re-layouts  0.45 us (3%)
    ppermute x5, starting transfers between devices, trade(): lax.ppermute(values, axis, [(i, i ^ mask) for i in range(lax.axis_size(ax...  9.29 us
    ppermute x5, waiting for transfers between devices, trade(): lax.ppermute(values, axis, [(i, i ^ mask) for i in range(lax.axis_size(ax...  2.54 us
    pallas_call x4, Pallas kernels, kernel_call(): pl.pallas_call(body, out_shape=outs, in_specs=[pl.BlockSpec(memory_space=...  2.12 us
    pallas_call x1, Pallas kernels, on_device(): pl.pallas_call(staged, out_shape=[jax.ShapeDtypeStruct((1,) + sky_alm.sha...  0.89 us
  transfers between devices with their start and end apart: 5, of which 3 were waited for; matrix products, arithmetic and copies ran while one was open for 3% of the time, Pallas kernels for 6%

profile of v2, /device:TPU:0, one launch (start us, length us, event | category | flops | bytes accessed | tf_op | source)
XLA Modules:
  0.0 15.4 jit_solution(3730583831982106584)
XLA Ops:
  0.0 0.0 copy-start
  0.0 0.9 %shard_map.64 = (bf16[1,2,3,2,128]{4,3,2,1,0:T(2,128)(2,1)S(1)}, bf16[70,4,128]{2,1,0:T(4,128)(2,1)S(1)}) custom-call(bf16[1,2,3,2,128]{4,3,2,1,0:T(2,128)(2,1)} %bitcast.21, bf16[6,4,128]{2,1,0:T(4,128)(2,1)} %bitcast.20, bf16[64,4,128]{2,1,0:T(4,128)(2,1)} %bitcast.19), custom_call_target="tpu_custom_call" | custom-call | tf_op jit(solution)/shard_map/pallas_call | solution.py:204
  0.9 2.5 %collective-permute-start = (bf16[1,2,3,2,128]{4,3,2,1,0:T(2,128)(2,1)S(1)}, bf16[1,2,3,2,128]{4,3,2,1,0:T(2,128)(2,1)S(1)}, u32[]{:S(2)}, u32[]{:S(2)}) collective-permute-start(bf16[1,2,3,2,128]{4,3,2,1,0:T(2,128)(2,1)S(1)} %get-tuple-element.11), channel_id=1, source_target_pairs={{0,20},{4,16},{8,28},{12,24},{16,4},{20,0},{24,12},{28,8},{1,21},{... | collective-permute-start | bytes 9224 | tf_op jit(solution)/shard_map/ppermute | solution.py:202
  3.4 1.6 %collective-permute-start.3 = (bf16[70,4,128]{2,1,0:T(4,128)(2,1)S(1)}, bf16[70,4,128]{2,1,0:T(4,128)(2,1)S(1)}, u32[]{:S(2)}, u32[]{:S(2)}) collective-permute-start(bf16[70,4,128]{2,1,0:T(4,128)(2,1)S(1)} %get-tuple-element.12.pack_ref), channel_id=1, source_target_pairs={{0,1},{1,0},{2,3},{3,2},{4,5},{5,4},{6,7},{7,6},{8,9},{9,8},{10,11... | collective-permute-start | bytes 215048 | tf_op jit(solution)/shard_map/ppermute | solution.py:202
  5.0 0.0 copy-start.2
  5.0 0.0 copy-start.1
  5.0 0.0 collective-permute-done
  5.0 1.7 %collective-permute-start.1 = (bf16[2,2,3,2,128]{4,3,2,1,0:T(2,128)(2,1)S(1)}, bf16[2,2,3,2,128]{4,3,2,1,0:T(2,128)(2,1)S(1)}, u32[]{:S(2)}, u32[]{:S(2)}) collective-permute-start(bf16[2,2,3,2,128]{4,3,2,1,0:T(2,128)(2,1)S(1)} %pad_maximum_fusion), channel_id=1, source_target_pairs={{0,12},{4,8},{8,4},{12,0},{16,28},{20,24},{24,20},{28,16},{1,13},{... | collective-permute-start | bytes 18440 | tf_op jit(solution)/shard_map/ppermute | solution.py:202
  6.8 1.4 %collective-permute-done.1 = bf16[2,2,3,2,128]{4,3,2,1,0:T(2,128)(2,1)S(1)} collective-permute-done((bf16[2,2,3,2,128]{4,3,2,1,0:T(2,128)(2,1)S(1)}, bf16[2,2,3,2,128]{4,3,2,1,0:T(2,128)(2,1)S(1)}, u32[]{:S(2)}, u32[]{:S(2)}) %collective-permute-start.1) | collective-permute-done | bytes 6176 | tf_op jit(solution)/shard_map/ppermute | solution.py:202
  8.2 0.5 %collective-permute-start.2 = (bf16[4,2,3,2,128]{4,3,2,1,0:T(2,128)(2,1)S(1)}, bf16[4,2,3,2,128]{4,3,2,1,0:T(2,128)(2,1)S(1)}, u32[]{:S(2)}, u32[]{:S(2)}) collective-permute-start(bf16[4,2,3,2,128]{4,3,2,1,0:T(2,128)(2,1)S(1)} %constant_dynamic-update-slice_fusion.near_ref), channel_id=1, source_target_pairs={{0,4},{4,0},{8,12},{12,8},{16,20},{20,16},{24,28},{28,24},{1,5},{5... | collective-permute-start | bytes 36872 | tf_op jit(solution)/shard_map/ppermute | solution.py:202
  8.6 0.0 copy-done.2
  8.6 0.0 copy-done.1
  8.6 0.1 dynamic-slice_bitcast_fusion
  8.7 0.8 %collective-permute-done.2.far_ref = bf16[4,2,3,2,128]{4,3,2,1,0:T(2,128)(2,1)S(1)} collective-permute-done((bf16[4,2,3,2,128]{4,3,2,1,0:T(2,128)(2,1)S(1)}, bf16[4,2,3,2,128]{4,3,2,1,0:T(2,128)(2,1)S(1)}, u32[]{:S(2)}, u32[]{:S(2)}) %collective-permute-start.2) | collective-permute-done | bytes 12320 | tf_op jit(solution)/shard_map/ppermute | solution.py:202
  9.5 0.0 collective-permute-done.3.pack_far_ref
  9.5 0.3 %shard_map.65.cube_ref = f32[16,128]{1,0:T(8,128)S(1)} custom-call(s32[1]{0:T(128)} %bitcast.place_ref, bf16[4,2,3,2,128]{4,3,2,1,0:T(2,128)(2,1)S(1)} %constant_dynamic-update-slice_fusion.near_ref, bf16[4,2,3,2,128]{4,3,2,1,0:T(2,128)(2,1)S(1)} %collective-permute-done.2.far_ref, bf16[70,4,128]{2,1,0:T(4,128)(2,1)S(1)} %get-tuple-element.12.pack_ref, ...), custom_call_target="tpu_custom_call" | custom-call | tf_op jit(solution)/shard_map/pallas_call | solution.py:23
  9.7 3.0 %collective-permute-start.4 = (f32[1,16,128]{2,1,0:T(8,128)S(1)}, f32[1,16,128]{2,1,0:T(8,128)S(1)}, u32[]{:S(2)}, u32[]{:S(2)}) collective-permute-start(f32[1,16,128]{2,1,0:T(8,128)S(1)} %bitcast.18), channel_id=1, source_target_pairs={{0,2},{1,3},{2,0},{3,1},{4,6},{5,7},{6,4},{7,5},{8,10},{9,11},{10,... | collective-permute-start | bytes 24584 | tf_op jit(solution)/shard_map/ppermute | solution.py:202
  12.8 0.0 copy-done
  12.8 0.1 dynamic-slice_bitcast_fusion.2
  12.9 0.1 reshape.35.theta_ref
  12.9 0.1 reshape.39.psi_ref
  13.0 0.1 reshape.37.phi_ref
  13.1 0.6 %shard_map.66 = (f32[16,1024]{1,0:T(8,128)S(1)}, f32[16,1024]{1,0:T(8,128)S(1)}, bf16[2,256,1024]{2,1,0:T(8,128)(2,1)S(1)}, bf16[2,256,1024]{2,1,0:T(8,128)(2,1)S(1)}) custom-call(s32[1]{0:T(128)} %bitcast.5.own_ref, s32[8,128]{1,0:T(8,128)S(1)} %reshape.35.theta_ref, s32[8,128]{1,0:T(8,128)S(1)} %reshape.37.phi_ref, s32[8,128]{1,0:T(8,128)S(1)} %reshape.39.psi_ref), custom_call_target="tpu_custom_call" | custom-call | tf_op jit(solution)/shard_map/pallas_call | solution.py:23
  13.7 0.3 %shard_map.67.near_ref = f32[8,128]{1,0:T(8,128)S(1)} custom-call(f32[16,128]{1,0:T(8,128)S(1)} %shard_map.65.cube_ref, f32[16,1024]{1,0:T(8,128)S(1)} %get-tuple-element.13.cos_ref, f32[16,1024]{1,0:T(8,128)S(1)} %get-tuple-element.14.sin_ref, bf16[2,256,1024]{2,1,0:T(8,128)(2,1)S(1)} %get-tuple-element.15.first_ref, ...), custom_call_target="tpu_custom_call" | custom-call | tf_op jit(solution)/shard_map/pallas_call | solution.py:23
  14.0 0.4 %collective-permute-done.4.cube_ref = f32[1,16,128]{2,1,0:T(8,128)S(1)} collective-permute-done((f32[1,16,128]{2,1,0:T(8,128)S(1)}, f32[1,16,128]{2,1,0:T(8,128)S(1)}, u32[]{:S(2)}, u32[]{:S(2)}) %collective-permute-start.4) | collective-permute-done | bytes 8224 | tf_op jit(solution)/shard_map/ppermute | solution.py:202
  14.4 1.0 %shard_map.68 = f32[16,64]{1,0:T(8,128)} custom-call(f32[1,16,128]{2,1,0:T(8,128)S(1)} %collective-permute-done.4.cube_ref, f32[16,1024]{1,0:T(8,128)S(1)} %get-tuple-element.13.cos_ref, f32[16,1024]{1,0:T(8,128)S(1)} %get-tuple-element.14.sin_ref, bf16[2,256,1024]{2,1,0:T(8,128)(2,1)S(1)} %get-tuple-element.15.first_ref, ...), custom_call_target="tpu_custom_call" | custom-call | tf_op jit(solution)/shard_map/pallas_call | solution.py:23
  (7 shorter events, 0.1 us)
Async XLA Ops:
  0.0 12.8 %copy-start = (s32[16,256]{1,0:T(8,128)S(1)}, s32[16,256]{1,0:T(8,128)}, u32[]{:S(2)}) copy-start(s32[16,256]{1,0:T(8,128)} %param.9) | copy-start | bytes 49156
  0.9 4.1 %collective-permute-start = (bf16[1,2,3,2,128]{4,3,2,1,0:T(2,128)(2,1)S(1)}, bf16[1,2,3,2,128]{4,3,2,1,0:T(2,128)(2,1)S(1)}, u32[]{:S(2)}, u32[]{:S(2)}) collective-permute-start(bf16[1,2,3,2,128]{4,3,2,1,0:T(2,128)(2,1)S(1)} %get-tuple-element.11), channel_id=1, source_target_pairs={{0,20},{4,16},{8,28},{12,24},{16,4},{20,0},{24,12},{28,8},{1,21},{... | collective-permute-start | bytes 9224 | tf_op jit(solution)/shard_map/ppermute | solution.py:202
  3.4 6.1 %collective-permute-start.3 = (bf16[70,4,128]{2,1,0:T(4,128)(2,1)S(1)}, bf16[70,4,128]{2,1,0:T(4,128)(2,1)S(1)}, u32[]{:S(2)}, u32[]{:S(2)}) collective-permute-start(bf16[70,4,128]{2,1,0:T(4,128)(2,1)S(1)} %get-tuple-element.12.pack_ref), channel_id=1, source_target_pairs={{0,1},{1,0},{2,3},{3,2},{4,5},{5,4},{6,7},{7,6},{8,9},{9,8},{10,11... | collective-permute-start | bytes 215048 | tf_op jit(solution)/shard_map/ppermute | solution.py:202
  5.0 3.6 %copy-start.2 = (s32[16,256]{1,0:T(8,128)S(1)}, s32[16,256]{1,0:T(8,128)}, u32[]{:S(2)}) copy-start(s32[16,256]{1,0:T(8,128)} %param.10) | copy-start | bytes 49156
  5.0 3.6 %copy-start.1 = (s32[16,256]{1,0:T(8,128)S(1)}, s32[16,256]{1,0:T(8,128)}, u32[]{:S(2)}) copy-start(s32[16,256]{1,0:T(8,128)} %param.11) | copy-start | bytes 49156
  5.0 3.1 %collective-permute-start.1 = (bf16[2,2,3,2,128]{4,3,2,1,0:T(2,128)(2,1)S(1)}, bf16[2,2,3,2,128]{4,3,2,1,0:T(2,128)(2,1)S(1)}, u32[]{:S(2)}, u32[]{:S(2)}) collective-permute-start(bf16[2,2,3,2,128]{4,3,2,1,0:T(2,128)(2,1)S(1)} %pad_maximum_fusion), channel_id=1, source_target_pairs={{0,12},{4,8},{8,4},{12,0},{16,28},{20,24},{24,20},{28,16},{1,13},{... | collective-permute-start | bytes 18440 | tf_op jit(solution)/shard_map/ppermute | solution.py:202
  8.2 1.3 %collective-permute-start.2 = (bf16[4,2,3,2,128]{4,3,2,1,0:T(2,128)(2,1)S(1)}, bf16[4,2,3,2,128]{4,3,2,1,0:T(2,128)(2,1)S(1)}, u32[]{:S(2)}, u32[]{:S(2)}) collective-permute-start(bf16[4,2,3,2,128]{4,3,2,1,0:T(2,128)(2,1)S(1)} %constant_dynamic-update-slice_fusion.near_ref), channel_id=1, source_target_pairs={{0,4},{4,0},{8,12},{12,8},{16,20},{20,16},{24,28},{28,24},{1,5},{5... | collective-permute-start | bytes 36872 | tf_op jit(solution)/shard_map/ppermute | solution.py:202
  9.7 4.7 %collective-permute-start.4 = (f32[1,16,128]{2,1,0:T(8,128)S(1)}, f32[1,16,128]{2,1,0:T(8,128)S(1)}, u32[]{:S(2)}, u32[]{:S(2)}) collective-permute-start(f32[1,16,128]{2,1,0:T(8,128)S(1)} %bitcast.18), channel_id=1, source_target_pairs={{0,2},{1,3},{2,0},{3,1},{4,6},{5,7},{6,4},{7,5},{8,10},{9,11},{10,... | collective-permute-start | bytes 24584 | tf_op jit(solution)/shard_map/ppermute | solution.py:202

commit v3 on v2

--- a/solution.py
+++ b/solution.py
@@ -18,25 +18,26 @@
 COS_TERMS = (1.0, -1 / 2, 1 / 24, -1 / 720, 1 / 40320)
 
 
-def kernel_call(body, outs, *args, scalars=1, flops=0):
+def kernel_call(body, outs, *args, scalars=1, flops=0, scratch=()):
     spaces = [pltpu.SMEM] * scalars + [pltpu.VMEM] * (len(args) - scalars)
     return pl.pallas_call(
         body,
         out_shape=outs,
         in_specs=[pl.BlockSpec(memory_space=space) for space in spaces],
         out_specs=jax.tree.map(lambda _: pl.BlockSpec(memory_space=pltpu.VMEM), outs),
+        scratch_shapes=list(scratch),
         cost_estimate=pl.CostEstimate(flops=flops, bytes_accessed=0, transcendentals=0),
         compiler_params=pltpu.CompilerParams(vmem_limit_bytes=16 << 20),
     )(*args)
 
 
-def staged(sky_ref, beam_ref, table_ref, sky_out, pack_out, sems):
-    rows = table_ref.shape[0]
-    copies = [
-        pltpu.make_async_copy(sky_ref, sky_out, sems.at[0]),
-        pltpu.make_async_copy(table_ref, pack_out.at[:rows], sems.at[1]),
-        pltpu.make_async_copy(beam_ref, pack_out.at[rows:], sems.at[2]),
-    ]
+def staged(*refs):
+    *given, out_ref, sems = refs
+    copies, start = [], 0
+    for i, ref in enumerate(given):
+        stop = start + ref.shape[0]
+        copies.append(pltpu.make_async_copy(ref, out_ref.at[start:stop], sems.at[i]))
+        start = stop
     for copy in copies:
         copy.start()
     for copy in copies:
@@ -58,14 +59,27 @@
     return jnp.where(swap != low, -c_abs, c_abs), jnp.where(low, -s_abs, s_abs)
 
 
-def features(cycles, planes, own_ref, theta_ref, phi_ref, psi_ref, cos_ref, sin_ref, first_ref, second_ref):
+def own_samples(ref, own, width):
+    values = pltpu.roll(ref[...], lax.rem(ref.shape[1] - own * width, ref.shape[1]), 1)[:, :LANES]
+    packed = LANES // width
+    rows = ref.shape[0] // packed
+    lane = lax.broadcasted_iota(jnp.int32, (rows, LANES), 1)
+    held = values[:rows]
+    for part in range(1, packed):
+        moved = pltpu.roll(values[part * rows : (part + 1) * rows], part * width, 1)
+        held = jnp.where(lane // width == part, moved, held)
+    return held
+
+
+def features(cycles, planes, width, own_ref, theta_ref, phi_ref, psi_ref, cos_ref, sin_ref, first_ref, second_ref):
     own = own_ref[0]
     modes = cos_ref.shape[0]
     halves = first_ref.shape[0]
     wide = 2 * planes
-    for row in range(theta_ref.shape[0]):
+    thetas, phis, psis = (own_samples(ref, own, width) for ref in (theta_ref, phi_ref, psi_ref))
+    for row in range(thetas.shape[0]):
         at = pl.ds(row * LANES, LANES)
-        theta, phi, psi = (ref[row : row + 1, :] for ref in (theta_ref, phi_ref, psi_ref))
+        theta, phi, psi = (values[row : row + 1] for values in (thetas, phis, psis))
         step = min(modes, 2 * SUBLANES)
 
         def turn_phi(first, at=at, phi=phi, step=step):
@@ -93,12 +107,14 @@
                 ref[half, :, at] = jnp.concatenate([high, high, low, jnp.zeros_like(low)], axis=0)
 
 
-def cubes(masks, cycles, place_ref, near_ref, far_ref, pack_ref, pack_far_ref, out_ref):
+def cubes(masks, cycles, place_ref, held_ref, b_ref, a_ref, c_ref, pack_ref, pack_far_ref, out_ref, sky_ref):
     place = place_ref[0]
     modes = out_ref.shape[0]
     planes = pack_ref.shape[1]
-    blocks, kinds, each = near_ref.shape[0], near_ref.shape[2], near_ref.shape[3]
+    blocks, kinds, each = held_ref.shape[0], held_ref.shape[2], held_ref.shape[3]
     f32 = jnp.float32
+    for i, ref in enumerate((held_ref, b_ref, a_ref, c_ref)):
+        sky_ref[i * blocks : (i + 1) * blocks] = ref[...]
 
     def both(row):
         return jnp.concatenate([pack_ref[row], pack_far_ref[row]], axis=0).astype(f32)
@@ -107,17 +123,7 @@
     rows = 2 * cycles * 2 * planes
 
     def one_mode(mode, block, inner, total):
-        sky = [
-            [
-                jnp.where(
-                    block < blocks,
-                    near_ref[block & (blocks - 1), k, c, inner : inner + 1, :],
-                    far_ref[block & (blocks - 1), k, c, inner : inner + 1, :],
-                ).astype(f32)
-                for c in range(kinds)
-            ]
-            for k in range(2)
-        ]
+        sky = [[sky_ref[block, k, c, inner : inner + 1, :].astype(f32) for c in range(kinds)] for k in range(2)]
         real = sum(sky[0][c] * beam[0][c] - sky[1][c] * beam[1][c] for c in range(kinds))
         imag = sum(sky[0][c] * beam[1][c] + sky[1][c] * beam[0][c] for c in range(kinds))
         spectra = [v.astype(jnp.bfloat16).astype(f32) for v in (real, imag)]
@@ -128,12 +134,17 @@
         return jnp.where(lane == mode % LANES, sums, total)
 
     def block_of(owner):
-        rest, block = owner ^ place, 0
+        rest, odd = owner ^ place, place & 1
+        low, high = (rest >> 1) & 1, (rest >> 2) & 1
+        crossed = odd ^ low
+        arrived = jnp.where(crossed == 0, jnp.where(odd == 0, 4, 6), jnp.where(odd == 0, 7, 5))
+        rest = rest ^ jnp.where(high == 1, arrived, 3 * low)
+        source = jnp.where(high == 1, 2 + crossed, low)
+        block = rest & 1
         for level, mask in enumerate(masks):
             bit = (rest >> (mask.bit_length() - 1)) & 1
-            rest = rest ^ (bit * mask)
-            block = block | (bit << level)
-        return block
+            block = (block ^ bit) | (bit << (level + 1))
+        return source * blocks + block
 
     for base in range(0, modes, LANES):
         count = min(modes, LANES)
@@ -192,76 +203,78 @@
     cycles, modes, planes, _ = wigner.shape
     detectors = theta_index.shape[0]
     width = theta_index.shape[1] // parts
-    packed = LANES // width
     samples = detectors * width
 
     def in_hbm(values):
         return pltpu.with_memory_space_constraint(values, pltpu.HBM)
 
-    def trade(values, axis, mask):
-        return lax.ppermute(values, axis, [(i, i ^ mask) for i in range(lax.axis_size(axis))])
-
-    sky, pack = pl.pallas_call(
+    def trade(values, det_mask, bm_mask=0, odd_mask=None):
+        pairs = []
+        for i in range(groups):
+            mask = odd_mask if odd_mask is not None and i % 2 else det_mask
+            pairs += [(i * parts + j, (i ^ mask) * parts + (j ^ bm_mask)) for j in range(parts)]
+        return lax.ppermute(values, ("det", "bm"), pairs)
+
+    given = [values.reshape((-1,) + wigner.shape[2:]) for values in (wigner, beam_blm, sky_alm)]
+    length = sum(values.shape[0] for values in given)
+    pack = pl.pallas_call(
         staged,
-        out_shape=[
-            jax.ShapeDtypeStruct((1,) + sky_alm.shape, bf16),
-            jax.ShapeDtypeStruct((cycles * modes + 2 * beam_blm.shape[1],) + wigner.shape[2:], bf16),
-        ],
+        out_shape=jax.ShapeDtypeStruct((length,) + wigner.shape[2:], bf16),
         in_specs=[pl.BlockSpec(memory_space=pltpu.HBM)] * 3,
-        out_specs=[pl.BlockSpec(memory_space=pltpu.VMEM)] * 2,
+        out_specs=pl.BlockSpec(memory_space=pltpu.VMEM),
         scratch_shapes=[pltpu.SemaphoreType.DMA((3,))],
         compiler_params=pltpu.CompilerParams(vmem_limit_bytes=16 << 20),
-    )(
-        in_hbm(sky_alm[None]),
-        in_hbm(beam_blm.reshape((-1,) + beam_blm.shape[2:])),
-        in_hbm(wigner.reshape((-1,) + wigner.shape[2:])),
-    )
-    masks = [(1 << level) | 1 for level in reversed(range(1, groups.bit_length() - 1))] + [1]
-    near = sky
-    far = trade(near, "det", masks[0])
-    pack_far = trade(pack, "bm", 1)
-    for mask in masks[1:]:
-        near = jnp.concatenate([near, far])
-        far = trade(near, "det", mask)
-
-    def columns(values):
-        held = lax.dynamic_slice_in_dim(values, own * width, width, 1)
-        return held.reshape(packed, detectors // packed, width).swapaxes(0, 1).reshape(-1, LANES)
+    )(*[in_hbm(values) for values in given])
+
+    def sky_of(values):
+        return values[length - given[2].shape[0] :].reshape((1,) + sky_alm.shape)
+
+    pack_near = trade(pack, 1)
+    pack_far = trade(pack, 1, 1)
+    held = jnp.concatenate([sky_of(pack), sky_of(pack_near)])
+    masks = [(1 << level) | 1 for level in range(3, groups.bit_length() - 1)]
+    for mask in masks:
+        held = jnp.concatenate([held, trade(held, mask)])
+    sky_a = trade(held, 4, odd_mask=6)
+    sky_b = trade(held, 3)
+    sky_c = trade(sky_a, 1)
 
     rows = 2 * cycles * 2 * planes
     factors = jax.ShapeDtypeStruct((parts // 2, 4 * rows, samples), bf16)
     waves = jax.ShapeDtypeStruct((modes, samples), f32)
     cosine, sine, first, second = kernel_call(
-        functools.partial(features, cycles, planes),
+        functools.partial(features, cycles, planes, width),
         [waves, waves, factors, factors],
         own.reshape(1),
-        columns(theta_index),
-        columns(phi_index),
-        columns(psi_index),
+        theta_index,
+        phi_index,
+        psi_index,
     )
     half = kernel_call(
         functools.partial(cubes, masks, cycles),
         jax.ShapeDtypeStruct((modes, 2 * rows), f32),
         place.reshape(1),
-        near,
-        far,
-        pack,
+        held,
+        sky_b,
+        sky_a,
+        sky_c,
+        pack_near,
         pack_far,
-    )
-    held, others, bit = half[None], [], 2
+        scratch=[pltpu.VMEM((groups,) + sky_alm.shape, bf16)],
+    )
+    far = trade(half, 1, 2)[None]
+    near = trade(half, 1)
+    bit = 4
     while bit < parts:
-        others.append(trade(held, "bm", bit))
-        if 2 * bit < parts:
-            held = jnp.concatenate([held, others[-1]])
+        far = jnp.concatenate([far, trade(jnp.concatenate([near[None], far]), 0, bit)])
         bit *= 2
     partial = kernel_call(
-        near_half, jax.ShapeDtypeStruct((samples // LANES, LANES), f32), half, cosine, sine, first, second, scalars=0
-    )
-    others = others[0] if len(others) == 1 else jnp.concatenate(others)
+        near_half, jax.ShapeDtypeStruct((samples // LANES, LANES), f32), near, cosine, sine, first, second, scalars=0
+    )
     return kernel_call(
         functools.partial(far_half, 1),
         jax.ShapeDtypeStruct((detectors, width), f32),
-        others,
+        far,
         cosine,
         sine,
         first,

time: 15.5 us -> 14.9 us (0.961)
  starting transfers between devices: 9.29 us -> 8.49 us
  waiting for transfers between devices: 2.54 us -> 3.09 us
  local copies, waits for them, and re-layouts: 0.45 us -> 0.02 us
    ppermute x5 -> x7, starting transfers between devices: 9.29 us -> 8.49 us  [trade(): return lax.ppermute(values, ('det', 'bm'), pairs)]
    ppermute x5 -> x7, waiting for transfers between devices: 2.54 us -> 3.09 us  [trade(): return lax.ppermute(values, ('det', 'bm'), pairs)]
    reshape x3 -> x0, local copies, waits for them, and re-layouts: 0.24 us -> none  [columns(): held.reshape(packed, detectors // packed, width).swapaxes(0, 1)]
    transpose x5 -> x0, local copies, waits for them, and re-layouts: 0.16 us -> none  [columns(): held.reshape(packed, detectors // packed, width).swapaxes(0, 1)]
  transfers between devices with their start and end apart: 5 -> 7, of which waited for: 3 -> 4; matrix products, arithmetic and copies ran while one was open for 3% -> 0% of each run, Pallas kernels for 6% -> 7%
where the time goes in v3:
time: 14.9 us; the launch traced here: 14.8 us
  starting transfers between devices  8.49 us (57%)
  Pallas kernels  3.11 us (21%)
  waiting for transfers between devices  3.09 us (21%)
    ppermute x7, starting transfers between devices, trade(): return lax.ppermute(values, ('det', 'bm'), pairs)  8.49 us
    ppermute x7, waiting for transfers between devices, trade(): return lax.ppermute(values, ('det', 'bm'), pairs)  3.09 us
    pallas_call x4, Pallas kernels, kernel_call(): pl.pallas_call(body, out_shape=outs, in_specs=[pl.BlockSpec(memory_space=...  2.24 us
    pallas_call x1, Pallas kernels, on_device(): pl.pallas_call(staged, out_shape=jax.ShapeDtypeStruct((length,) + wigner....  0.87 us
  transfers between devices with their start and end apart: 7, of which 4 were waited for; matrix products, arithmetic and copies ran while one was open for 0% of the time, Pallas kernels for 7%

profile of v3, /device:TPU:0, one launch (start us, length us, event | category | flops | bytes accessed | tf_op | source)
XLA Modules:
  0.0 14.8 jit_solution(3813198537907704119)
XLA Ops:
  0.0 0.9 %shard_map.64 = bf16[73,4,128]{2,1,0:T(4,128)(2,1)S(1)} custom-call(bf16[64,4,128]{2,1,0:T(4,128)(2,1)} %bitcast.9, bf16[6,4,128]{2,1,0:T(4,128)(2,1)} %bitcast.12, bf16[3,4,128]{2,1,0:T(4,128)(2,1)} %bitcast.13), custom_call_target="tpu_custom_call" | custom-call | tf_op jit(solution)/shard_map/pallas_call | solution.py:220
  0.9 0.6 %collective-permute-start = (bf16[73,4,128]{2,1,0:T(4,128)(2,1)S(1)}, bf16[73,4,128]{2,1,0:T(4,128)(2,1)S(1)}, u32[]{:S(2)}, u32[]{:S(2)}) collective-permute-start(bf16[73,4,128]{2,1,0:T(4,128)(2,1)S(1)} %shard_map.64), channel_id=1, source_target_pairs={{0,4},{1,5},{2,6},{3,7},{4,0},{5,1},{6,2},{7,3},{8,12},{9,13},{10,... | collective-permute-start | bytes 224264 | tf_op jit(solution)/shard_map/ppermute | solution.py:216
  1.4 2.7 %collective-permute-start.4 = (bf16[73,4,128]{2,1,0:T(4,128)(2,1)S(1)}, bf16[73,4,128]{2,1,0:T(4,128)(2,1)S(1)}, u32[]{:S(2)}, u32[]{:S(2)}) collective-permute-start(bf16[73,4,128]{2,1,0:T(4,128)(2,1)S(1)} %shard_map.64), channel_id=1, source_target_pairs={{0,5},{1,4},{2,7},{3,6},{4,1},{5,0},{6,3},{7,2},{8,13},{9,12},{10,... | collective-permute-start | bytes 224264 | tf_op jit(solution)/shard_map/ppermute | solution.py:216
  4.1 0.0 collective-permute-done.pack_ref
  4.1 1.6 %collective-permute-start.2 = (bf16[2,2,3,2,128]{4,3,2,1,0:T(2,128)(2,1)S(1)}, bf16[2,2,3,2,128]{4,3,2,1,0:T(2,128)(2,1)S(1)}, u32[]{:S(2)}, u32[]{:S(2)}) collective-permute-start(bf16[2,2,3,2,128]{4,3,2,1,0:T(2,128)(2,1)S(1)} %pad_maximum_fusion.held_ref), channel_id=1, source_target_pairs={{0,16},{1,17},{2,18},{3,19},{4,28},{5,29},{6,30},{7,31},{8,24},{9,... | collective-permute-start | bytes 18440 | tf_op jit(solution)/shard_map/ppermute | solution.py:216
  5.7 0.9 %collective-permute-start.1 = (bf16[2,2,3,2,128]{4,3,2,1,0:T(2,128)(2,1)S(1)}, bf16[2,2,3,2,128]{4,3,2,1,0:T(2,128)(2,1)S(1)}, u32[]{:S(2)}, u32[]{:S(2)}) collective-permute-start(bf16[2,2,3,2,128]{4,3,2,1,0:T(2,128)(2,1)S(1)} %pad_maximum_fusion.held_ref), channel_id=1, source_target_pairs={{0,12},{1,13},{2,14},{3,15},{4,8},{5,9},{6,10},{7,11},{8,4},{9,5},... | collective-permute-start | bytes 18440 | tf_op jit(solution)/shard_map/ppermute | solution.py:216
  6.6 1.3 %collective-permute-done.2.a_ref = bf16[2,2,3,2,128]{4,3,2,1,0:T(2,128)(2,1)S(1)} collective-permute-done((bf16[2,2,3,2,128]{4,3,2,1,0:T(2,128)(2,1)S(1)}, bf16[2,2,3,2,128]{4,3,2,1,0:T(2,128)(2,1)S(1)}, u32[]{:S(2)}, u32[]{:S(2)}) %collective-permute-start.2) | collective-permute-done | bytes 6176 | tf_op jit(solution)/shard_map/ppermute | solution.py:216
  7.8 0.0 collective-permute-start.3
  7.9 0.0 collective-permute-done.4.pack_far_ref
  7.9 0.9 %collective-permute-done.1.b_ref = bf16[2,2,3,2,128]{4,3,2,1,0:T(2,128)(2,1)S(1)} collective-permute-done((bf16[2,2,3,2,128]{4,3,2,1,0:T(2,128)(2,1)S(1)}, bf16[2,2,3,2,128]{4,3,2,1,0:T(2,128)(2,1)S(1)}, u32[]{:S(2)}, u32[]{:S(2)}) %collective-permute-start.1) | collective-permute-done | bytes 6176 | tf_op jit(solution)/shard_map/ppermute | solution.py:216
  8.8 0.2 %collective-permute-done.3.c_ref = bf16[2,2,3,2,128]{4,3,2,1,0:T(2,128)(2,1)S(1)} collective-permute-done((bf16[2,2,3,2,128]{4,3,2,1,0:T(2,128)(2,1)S(1)}, bf16[2,2,3,2,128]{4,3,2,1,0:T(2,128)(2,1)S(1)}, u32[]{:S(2)}, u32[]{:S(2)}) %collective-permute-start.3) | collective-permute-done | bytes 6176 | tf_op jit(solution)/shard_map/ppermute | solution.py:216
  9.0 0.0 copy-start
  9.0 0.0 copy-start.1
  9.0 0.0 copy-start.2
  9.0 0.3 %shard_map.65 = f32[16,128]{1,0:T(8,128)S(1)} custom-call(s32[1]{0:T(128)} %bitcast.place_ref, bf16[2,2,3,2,128]{4,3,2,1,0:T(2,128)(2,1)S(1)} %pad_maximum_fusion.held_ref, bf16[2,2,3,2,128]{4,3,2,1,0:T(2,128)(2,1)S(1)} %collective-permute-done.1.b_ref, bf16[2,2,3,2,128]{4,3,2,1,0:T(2,128)(2,1)S(1)} %collective-permute-done.2.a_ref, ...), custom_call_target="tpu_custom_call" | custom-call | tf_op jit(solution)/shard_map/pallas_call | solution.py:23
  9.3 0.5 %collective-permute-start.6 = (f32[16,128]{1,0:T(8,128)S(1)}, f32[16,128]{1,0:T(8,128)S(1)}, u32[]{:S(2)}, u32[]{:S(2)}) collective-permute-start(f32[16,128]{1,0:T(8,128)S(1)} %shard_map.65), channel_id=1, source_target_pairs={{0,4},{1,5},{2,6},{3,7},{4,0},{5,1},{6,2},{7,3},{8,12},{9,13},{10,... | collective-permute-start | bytes 24584 | tf_op jit(solution)/shard_map/ppermute | solution.py:216
  9.8 2.3 %collective-permute-start.5 = (f32[16,128]{1,0:T(8,128)S(1)}, f32[16,128]{1,0:T(8,128)S(1)}, u32[]{:S(2)}, u32[]{:S(2)}) collective-permute-start(f32[16,128]{1,0:T(8,128)S(1)} %shard_map.65), channel_id=1, source_target_pairs={{0,6},{1,7},{2,4},{3,5},{4,2},{5,3},{6,0},{7,1},{8,14},{9,15},{10,... | collective-permute-start | bytes 24584 | tf_op jit(solution)/shard_map/ppermute | solution.py:216
  12.1 0.0 copy-done
  12.1 0.0 copy-done.1
  12.1 0.0 copy-done.2
  12.1 0.7 %shard_map.66 = (f32[16,1024]{1,0:T(8,128)S(1)}, f32[16,1024]{1,0:T(8,128)S(1)}, bf16[2,256,1024]{2,1,0:T(8,128)(2,1)S(1)}, bf16[2,256,1024]{2,1,0:T(8,128)(2,1)S(1)}) custom-call(s32[1]{0:T(128)} %bitcast.7.own_ref, s32[16,256]{1,0:T(8,128)S(1)} %copy-done, s32[16,256]{1,0:T(8,128)S(1)} %copy-done.1, s32[16,256]{1,0:T(8,128)S(1)} %copy-done.2), custom_call_target="tpu_custom_call" | custom-call | tf_op jit(solution)/shard_map/pallas_call | solution.py:23
  12.9 0.0 collective-permute-done.6.cube_ref
  12.9 0.3 %shard_map.67.near_ref = f32[8,128]{1,0:T(8,128)S(1)} custom-call(f32[16,128]{1,0:T(8,128)S(1)} %collective-permute-done.6.cube_ref, f32[16,1024]{1,0:T(8,128)S(1)} %get-tuple-element.9.cos_ref, f32[16,1024]{1,0:T(8,128)S(1)} %get-tuple-element.10.sin_ref, bf16[2,256,1024]{2,1,0:T(8,128)(2,1)S(1)} %get-tuple-element.11.first_ref, ...), custom_call_target="tpu_custom_call" | custom-call | tf_op jit(solution)/shard_map/pallas_call | solution.py:23
  13.1 0.7 %collective-permute-done.5 = f32[16,128]{1,0:T(8,128)S(1)} collective-permute-done((f32[16,128]{1,0:T(8,128)S(1)}, f32[16,128]{1,0:T(8,128)S(1)}, u32[]{:S(2)}, u32[]{:S(2)}) %collective-permute-start.5) | collective-permute-done | bytes 8224 | tf_op jit(solution)/shard_map/ppermute | solution.py:216
  13.8 1.0 %shard_map.68 = f32[16,64]{1,0:T(8,128)} custom-call(f32[1,16,128]{2,1,0:T(8,128)S(1)} %bitcast.8, f32[16,1024]{1,0:T(8,128)S(1)} %get-tuple-element.9.cos_ref, f32[16,1024]{1,0:T(8,128)S(1)} %get-tuple-element.10.sin_ref, bf16[2,256,1024]{2,1,0:T(8,128)(2,1)S(1)} %get-tuple-element.11.first_ref, bf16[2,256,1024]{2,1,0:T(8,128)(2,1)S(1)} %get-tuple-element.12.second_ref, ...), custom_call_target="tpu_custom_call" | custom-call | tf_op jit(solution)/shard_map/pallas_call | solution.py:23
  (3 shorter events, 0.0 us)
Async XLA Ops:
  0.9 3.2 %collective-permute-start = (bf16[73,4,128]{2,1,0:T(4,128)(2,1)S(1)}, bf16[73,4,128]{2,1,0:T(4,128)(2,1)S(1)}, u32[]{:S(2)}, u32[]{:S(2)}) collective-permute-start(bf16[73,4,128]{2,1,0:T(4,128)(2,1)S(1)} %shard_map.64), channel_id=1, source_target_pairs={{0,4},{1,5},{2,6},{3,7},{4,0},{5,1},{6,2},{7,3},{8,12},{9,13},{10,... | collective-permute-start | bytes 224264 | tf_op jit(solution)/shard_map/ppermute | solution.py:216
  1.4 6.4 %collective-permute-start.4 = (bf16[73,4,128]{2,1,0:T(4,128)(2,1)S(1)}, bf16[73,4,128]{2,1,0:T(4,128)(2,1)S(1)}, u32[]{:S(2)}, u32[]{:S(2)}) collective-permute-start(bf16[73,4,128]{2,1,0:T(4,128)(2,1)S(1)} %shard_map.64), channel_id=1, source_target_pairs={{0,5},{1,4},{2,7},{3,6},{4,1},{5,0},{6,3},{7,2},{8,13},{9,12},{10,... | collective-permute-start | bytes 224264 | tf_op jit(solution)/shard_map/ppermute | solution.py:216
  4.1 3.7 %collective-permute-start.2 = (bf16[2,2,3,2,128]{4,3,2,1,0:T(2,128)(2,1)S(1)}, bf16[2,2,3,2,128]{4,3,2,1,0:T(2,128)(2,1)S(1)}, u32[]{:S(2)}, u32[]{:S(2)}) collective-permute-start(bf16[2,2,3,2,128]{4,3,2,1,0:T(2,128)(2,1)S(1)} %pad_maximum_fusion.held_ref), channel_id=1, source_target_pairs={{0,16},{1,17},{2,18},{3,19},{4,28},{5,29},{6,30},{7,31},{8,24},{9,... | collective-permute-start | bytes 18440 | tf_op jit(solution)/shard_map/ppermute | solution.py:216
  5.7 3.1 %collective-permute-start.1 = (bf16[2,2,3,2,128]{4,3,2,1,0:T(2,128)(2,1)S(1)}, bf16[2,2,3,2,128]{4,3,2,1,0:T(2,128)(2,1)S(1)}, u32[]{:S(2)}, u32[]{:S(2)}) collective-permute-start(bf16[2,2,3,2,128]{4,3,2,1,0:T(2,128)(2,1)S(1)} %pad_maximum_fusion.held_ref), channel_id=1, source_target_pairs={{0,12},{1,13},{2,14},{3,15},{4,8},{5,9},{6,10},{7,11},{8,4},{9,5},... | collective-permute-start | bytes 18440 | tf_op jit(solution)/shard_map/ppermute | solution.py:216
  7.8 1.2 %collective-permute-start.3 = (bf16[2,2,3,2,128]{4,3,2,1,0:T(2,128)(2,1)S(1)}, bf16[2,2,3,2,128]{4,3,2,1,0:T(2,128)(2,1)S(1)}, u32[]{:S(2)}, u32[]{:S(2)}) collective-permute-start(bf16[2,2,3,2,128]{4,3,2,1,0:T(2,128)(2,1)S(1)} %collective-permute-done.2.a_ref), channel_id=1, source_target_pairs={{0,4},{1,5},{2,6},{3,7},{4,0},{5,1},{6,2},{7,3},{8,12},{9,13},{10,... | collective-permute-start | bytes 18440 | tf_op jit(solution)/shard_map/ppermute | solution.py:216
  9.0 3.1 %copy-start = (s32[16,256]{1,0:T(8,128)S(1)}, s32[16,256]{1,0:T(8,128)}, u32[]{:S(2)}) copy-start(s32[16,256]{1,0:T(8,128)} %theta_ref.1) | copy-start | bytes 49156
  9.0 3.1 %copy-start.1 = (s32[16,256]{1,0:T(8,128)S(1)}, s32[16,256]{1,0:T(8,128)}, u32[]{:S(2)}) copy-start(s32[16,256]{1,0:T(8,128)} %phi_ref.1) | copy-start | bytes 49156
  9.0 3.1 %copy-start.2 = (s32[16,256]{1,0:T(8,128)S(1)}, s32[16,256]{1,0:T(8,128)}, u32[]{:S(2)}) copy-start(s32[16,256]{1,0:T(8,128)} %psi_ref.1) | copy-start | bytes 49156
  9.3 3.6 %collective-permute-start.6 = (f32[16,128]{1,0:T(8,128)S(1)}, f32[16,128]{1,0:T(8,128)S(1)}, u32[]{:S(2)}, u32[]{:S(2)}) collective-permute-start(f32[16,128]{1,0:T(8,128)S(1)} %shard_map.65), channel_id=1, source_target_pairs={{0,4},{1,5},{2,6},{3,7},{4,0},{5,1},{6,2},{7,3},{8,12},{9,13},{10,... | collective-permute-start | bytes 24584 | tf_op jit(solution)/shard_map/ppermute | solution.py:216
  9.8 4.0 %collective-permute-start.5 = (f32[16,128]{1,0:T(8,128)S(1)}, f32[16,128]{1,0:T(8,128)S(1)}, u32[]{:S(2)}, u32[]{:S(2)}) collective-permute-start(f32[16,128]{1,0:T(8,128)S(1)} %shard_map.65), channel_id=1, source_target_pairs={{0,6},{1,7},{2,4},{3,5},{4,2},{5,3},{6,0},{7,1},{8,14},{9,15},{10,... | collective-permute-start | bytes 24584 | tf_op jit(solution)/shard_map/ppermute | solution.py:216

commit v4 on v3

v4 whole, which is shorter than its diff:
```python
import functools
import math

import jax
import jax.numpy as jnp
from jax import lax
from jax.experimental import pallas as pl
from jax.experimental.pallas import tpu as pltpu
from jax.sharding import PartitionSpec as P


NPHI = 16384
NPSI = 32
LANES = 128
SUBLANES = 8

SIN_TERMS = (1.0, -1 / 6, 1 / 120, -1 / 5040, 1 / 362880)
COS_TERMS = (1.0, -1 / 2, 1 / 24, -1 / 720, 1 / 40320)


def kernel_call(body, outs, *args, scalars=1, flops=0, scratch=()):
    spaces = [pltpu.SMEM] * scalars + [pltpu.VMEM] * (len(args) - scalars)
    return pl.pallas_call(
        body,
        out_shape=outs,
        in_specs=[pl.BlockSpec(memory_space=space) for space in spaces],
        out_specs=jax.tree.map(lambda _: pl.BlockSpec(memory_space=pltpu.VMEM), outs),
        scratch_shapes=list(scratch),
        cost_estimate=pl.CostEstimate(flops=flops, bytes_accessed=0, transcendentals=0),
        compiler_params=pltpu.CompilerParams(vmem_limit_bytes=16 << 20),
    )(*args)


def staged(*refs):
    *given, out_ref, sems = refs
    copies, start = [], 0
    for i, ref in enumerate(given):
        stop = start + ref.shape[0]
        copies.append(pltpu.make_async_copy(ref, out_ref.at[start:stop], sems.at[i]))
        start = stop
    for copy in copies:
        copy.start()
    for copy in copies:
        copy.wait()


def cos_sin(steps, period):
    quarter = steps.astype(jnp.float32) * (4.0 / period)
    nearest = jnp.floor(quarter + 0.5)
    angle = (quarter - nearest) * (math.pi / 2)
    square = angle * angle
    sine, cosine = SIN_TERMS[-1], COS_TERMS[-1]
    for s_term, c_term in zip(SIN_TERMS[-2::-1], COS_TERMS[-2::-1]):
        sine, cosine = sine * square + s_term, cosine * square + c_term
    sine = sine * angle
    turn = nearest.astype(jnp.int32)
    swap, low = (turn & 1) == 1, (turn & 2) == 2
    c_abs, s_abs = jnp.where(swap, sine, cosine), jnp.where(swap, cosine, sine)
    return jnp.where(swap != low, -c_abs, c_abs), jnp.where(low, -s_abs, s_abs)


def own_samples(ref, own, width):
    values = pltpu.roll(ref[...], lax.rem(ref.shape[1] - own * width, ref.shape[1]), 1)[:, :LANES]
    packed = LANES // width
    rows = ref.shape[0] // packed
    lane = lax.broadcasted_iota(jnp.int32, (rows, LANES), 1)
    held = values[:rows]
    for part in range(1, packed):
        moved = pltpu.roll(values[part * rows : (part + 1) * rows], part * width, 1)
        held = jnp.where(lane // width == part, moved, held)
    return held


def features(cycles, planes, width, own_ref, theta_ref, phi_ref, psi_ref, cos_ref, sin_ref, factor_ref):
    own = own_ref[0]
    modes = cos_ref.shape[0]
    wide = 2 * planes
    halves = factor_ref.shape[0] // (4 * cycles * wide)
    thetas, phis, psis = (own_samples(ref, own, width) for ref in (theta_ref, phi_ref, psi_ref))
    for row in range(thetas.shape[0]):
        at = pl.ds(row * LANES, LANES)
        theta, phi, psi = (values[row : row + 1] for values in (thetas, phis, psis))
        step = min(modes, 2 * SUBLANES)

        def turn_phi(first, at=at, phi=phi, step=step):
            mode = first + lax.broadcasted_iota(jnp.int32, (step, LANES), 0)
            c, s = cos_sin((mode * phi) & (NPHI - 1), NPHI)
            cos_ref[pl.ds(first, step), at] = c
            sin_ref[pl.ds(first, step), at] = s

        if modes == step:
            turn_phi(0)
        else:
            pl.loop(0, modes, step=step)(turn_phi)
        chosen = [theta == cycle for cycle in range(cycles)]
        firsts, seconds = [], []
        for half in range(halves):
            inner = lax.broadcasted_iota(jnp.int32, (wide, LANES), 0)
            part = (own ^ (2 * half)) ^ (inner // planes)
            plane = part * planes + inner % planes
            c, s = cos_sin((plane * psi) & (NPSI - 1), NPSI)
            for pick in chosen:
                c_own, s_own = jnp.where(pick, c, 0.0), jnp.where(pick, s, 0.0)
                firsts += [c_own, -s_own]
                seconds += [s_own, c_own]
        for i, rows in enumerate((firsts, seconds)):
            full = jnp.concatenate(rows, axis=0)
            high = full.astype(jnp.bfloat16)
            low = (full - high.astype(jnp.float32)).astype(jnp.bfloat16)
            factor_ref[:, pl.ds((2 * row + i) * LANES, LANES)] = jnp.concatenate([high, low], axis=0)


def cubes(masks, shape, sources, place_ref, pack_ref, pack_far_ref, *refs):
    cycles, modes, planes = shape
    *refs, out_ref = refs
    place = place_ref[0]
    blocks, kinds, each = refs[0].shape[0], refs[0].shape[2], refs[0].shape[3]
    rows, width = 2 * cycles * 2 * planes, max(modes, LANES)
    f32 = jnp.float32
    lane = lax.broadcasted_iota(jnp.int32, (rows, width), 1)

    def both(row):
        return jnp.concatenate([pack_ref[row], pack_far_ref[row]], axis=0).astype(f32)

    beam = [[both(cycles * modes + k * kinds + c) for c in range(kinds)] for k in range(2)]

    def one_mode(mode, sky, total):
        real = sum(sky[0][c] * beam[0][c] - sky[1][c] * beam[1][c] for c in range(kinds))
        imag = sum(sky[0][c] * beam[1][c] + sky[1][c] * beam[0][c] for c in range(kinds))
        spectra = [v.astype(jnp.bfloat16).astype(f32) for v in (real, imag)]
        tables = [both(g * modes + mode) for g in range(cycles)]
        products = jnp.concatenate([s * t for t in tables for s in spectra], axis=0)
        return jnp.where(lane == mode, jnp.sum(products, axis=1, keepdims=True), total)

    def one_block(ref, sender, block, total):
        owner = sender ^ (block & 1)
        for level, mask in enumerate(masks):
            owner = owner ^ (((block >> (level + 1)) & 1) * mask)
        for inner in range(each):
            sky = [[ref[block, k, c, inner : inner + 1, :].astype(f32) for c in range(kinds)] for k in range(2)]
            total = one_mode(owner * each + inner, sky, total)
        return total

    total = refs[-1][...] if len(refs) > len(sources) else jnp.zeros((rows, width), f32)
    for ref, (even, odd) in zip(refs, sources):
        sender = place ^ jnp.where(place & 1 == 1, odd, even)
        if blocks <= SUBLANES:
            for block in range(blocks):
                total = one_block(ref, sender, block, total)
        else:
            total = lax.fori_loop(0, blocks, functools.partial(one_block, ref, sender), total)
    if out_ref.shape[0] == modes:
        for base in range(0, width, LANES):
            part = total[:, base : base + LANES]
            count = min(modes - base, LANES)
            out_ref[base : base + count, :] = jnp.concatenate([part, part], axis=0).T[:count]
    else:
        out_ref[...] = total


def sampled(near_ref, far_ref, cos_ref, sin_ref, factor_ref, out_ref):
    width = out_ref.shape[1]
    halves = [ref[half] for ref in (near_ref, far_ref) for half in range(ref.shape[0])]
    modes, doubled = halves[0].shape
    lane = lax.broadcasted_iota(jnp.int32, (modes, doubled), 1)
    whole = [jnp.where(lane < doubled // 2, *halves[i : i + 2]) for i in range(0, len(halves), 2)]
    high = [v.astype(jnp.bfloat16) for v in whole]
    low = [(v - h.astype(jnp.float32)).astype(jnp.bfloat16) for v, h in zip(whole, high)]
    left = jnp.concatenate(
        [jnp.concatenate(high + high, axis=1), jnp.concatenate(low + [jnp.zeros_like(v) for v in low], axis=1)], axis=0
    )
    done = []
    for row in range(out_ref.shape[0] * width // LANES):
        at = pl.ds(row * LANES, LANES)
        both = jnp.dot(left, factor_ref[:, pl.ds(2 * row * LANES, 2 * LANES)], preferred_element_type=jnp.float32)
        both = both[:modes] + both[modes:]
        done.append(jnp.sum(both[:, :LANES] * cos_ref[:, at] - both[:, LANES:] * sin_ref[:, at], axis=0, keepdims=True))
    result = jnp.concatenate(done, axis=0)
    rows = result.shape[0]
    for part in range(LANES // width):
        out_ref[part * rows : (part + 1) * rows, :] = result[:, part * width : (part + 1) * width]


def on_device(sky_alm, beam_blm, wigner, theta_index, phi_index, psi_index):
    f32, bf16 = jnp.float32, jnp.bfloat16
    groups, parts = lax.axis_size("det"), lax.axis_size("bm")
    place, own = lax.axis_index("det"), lax.axis_index("bm")
    cycles, modes, planes, _ = wigner.shape
    detectors = theta_index.shape[0]
    width = theta_index.shape[1] // parts
    samples = detectors * width

    def in_hbm(values):
        return pltpu.with_memory_space_constraint(values, pltpu.HBM)

    def trade(values, det_mask, bm_mask=0, odd_mask=None):
        pairs = []
        for i in range(groups):
            mask = odd_mask if odd_mask is not None and i % 2 else det_mask
            pairs += [(i * parts + j, (i ^ mask) * parts + (j ^ bm_mask)) for j in range(parts)]
        return lax.ppermute(values, ("det", "bm"), pairs)

    given = [values.reshape((-1,) + wigner.shape[2:]) for values in (wigner, beam_blm, sky_alm)]
    length = sum(values.shape[0] for values in given)
    pack = pl.pallas_call(
        staged,
        out_shape=jax.ShapeDtypeStruct((length,) + wigner.shape[2:], bf16),
        in_specs=[pl.BlockSpec(memory_space=pltpu.HBM)] * 3,
        out_specs=pl.BlockSpec(memory_space=pltpu.VMEM),
        scratch_shapes=[pltpu.SemaphoreType.DMA((3,))],
        compiler_params=pltpu.CompilerParams(vmem_limit_bytes=16 << 20),
    )(*[in_hbm(values) for values in given])

    def sky_of(values):
        return values[length - given[2].shape[0] :].reshape((1,) + sky_alm.shape)

    pack_near = trade(pack, 1)
    pack_far = trade(pack, 1, 1)
    held = jnp.concatenate([sky_of(pack), sky_of(pack_near)])
    masks = [(1 << level) | 1 for level in range(3, groups.bit_length() - 1)]
    for mask in masks:
        held = jnp.concatenate([held, trade(held, mask)])
    sky_a = trade(held, 4, odd_mask=6)
    sky_b = trade(held, 3)
    sky_c = trade(sky_a, 1)

    rows = 2 * cycles * 2 * planes
    factors = jax.ShapeDtypeStruct((2 * parts // 2 * rows, 2 * samples), bf16)
    waves = jax.ShapeDtypeStruct((modes, samples), f32)
    factors_of = kernel_call(
        functools.partial(features, cycles, planes, width),
        [waves, waves, factors],
        own.reshape(1),
        theta_index,
        phi_index,
        psi_index,
    )

    def half_cube(outs, sources, *skies):
        return kernel_call(
            functools.partial(cubes, masks, (cycles, modes, planes), sources), outs, place.reshape(1), pack_near, pack_far, *skies
        )

    columns = jax.ShapeDtypeStruct((rows, max(modes, LANES)), f32)
    half = half_cube(columns, ((0, 0), (4, 6)), held, sky_a)
    half = half_cube(jax.ShapeDtypeStruct((modes, 2 * rows), f32), ((3, 3), (7, 5)), sky_b, sky_c, half)
    far = trade(half, 1, 2)[None]
    near = trade(half, 1)[None]
    bit = 4
    while bit < parts:
        far = jnp.concatenate([far, trade(jnp.concatenate([near, far]), 0, bit)])
        bit *= 2
    return kernel_call(
        sampled,
        jax.ShapeDtypeStruct((detectors, width), f32),
        near,
        far,
        *factors_of,
        scalars=0,
    )


def solution(mesh):
    placed = (
        P(None, None, "det", None),
        P(None, None, "bm", None),
        P("det", None, "bm", None),
        P("det", None),
        P("det", None),
        P("det", None),
    )
    return jax.shard_map(
        on_device, mesh=mesh, in_specs=placed, out_specs=P("det", "bm"), check_vma=False
    )
```

time: 14.9 us -> 14.5 us (0.973)
  Pallas kernels: 3.11 us -> 2.77 us
    pallas_call x4, Pallas kernels: 2.24 us -> 1.9 us  [kernel_call(): pl.pallas_call(body, out_shape=outs, in_specs=[pl.BlockSpec(memory_space=...]
  transfers between devices with their start and end apart: 7 -> 7, of which waited for: 4 -> 4; matrix products, arithmetic and copies ran while one was open for 0% -> 0% of each run, Pallas kernels for 7% -> 5%
where the time goes in v4:
time: 14.5 us; the launch traced here: 14.3 us
  starting transfers between devices  8.43 us (58%)
  waiting for transfers between devices  3.03 us (21%)
  Pallas kernels  2.77 us (19%)
    ppermute x7, starting transfers between devices, trade(): return lax.ppermute(values, ('det', 'bm'), pairs)  8.43 us
    ppermute x7, waiting for transfers between devices, trade(): return lax.ppermute(values, ('det', 'bm'), pairs)  3.03 us
    pallas_call x4, Pallas kernels, kernel_call(): pl.pallas_call(body, out_shape=outs, in_specs=[pl.BlockSpec(memory_space=...  1.9 us
    pallas_call x1, Pallas kernels, on_device(): pl.pallas_call(staged, out_shape=jax.ShapeDtypeStruct((length,) + wigner....  0.87 us
  transfers between devices with their start and end apart: 7, of which 4 were waited for; matrix products, arithmetic and copies ran while one was open for 0% of the time, Pallas kernels for 5%

profile of v4, /device:TPU:0, one launch (start us, length us, event | category | flops | bytes accessed | tf_op | source)
XLA Modules:
  0.0 14.3 jit_solution(15040422383300429563)
XLA Ops:
  0.0 0.9 %shard_map.64 = bf16[73,4,128]{2,1,0:T(4,128)(2,1)S(1)} custom-call(bf16[64,4,128]{2,1,0:T(4,128)(2,1)} %bitcast.11, bf16[6,4,128]{2,1,0:T(4,128)(2,1)} %bitcast.14, bf16[3,4,128]{2,1,0:T(4,128)(2,1)} %bitcast.15), custom_call_target="tpu_custom_call" | custom-call | tf_op jit(solution)/shard_map/pallas_call | solution.py:205
  0.9 0.6 %collective-permute-start = (bf16[73,4,128]{2,1,0:T(4,128)(2,1)S(1)}, bf16[73,4,128]{2,1,0:T(4,128)(2,1)S(1)}, u32[]{:S(2)}, u32[]{:S(2)}) collective-permute-start(bf16[73,4,128]{2,1,0:T(4,128)(2,1)S(1)} %shard_map.64), channel_id=1, source_target_pairs={{0,4},{1,5},{2,6},{3,7},{4,0},{5,1},{6,2},{7,3},{8,12},{9,13},{10,... | collective-permute-start | bytes 224264 | tf_op jit(solution)/shard_map/ppermute | solution.py:201
  1.4 2.7 %collective-permute-start.1 = (bf16[73,4,128]{2,1,0:T(4,128)(2,1)S(1)}, bf16[73,4,128]{2,1,0:T(4,128)(2,1)S(1)}, u32[]{:S(2)}, u32[]{:S(2)}) collective-permute-start(bf16[73,4,128]{2,1,0:T(4,128)(2,1)S(1)} %shard_map.64), channel_id=1, source_target_pairs={{0,5},{1,4},{2,7},{3,6},{4,1},{5,0},{6,3},{7,2},{8,13},{9,12},{10,... | collective-permute-start | bytes 224264 | tf_op jit(solution)/shard_map/ppermute | solution.py:201
  4.1 0.0 collective-permute-done.pack_ref
  4.1 1.6 %collective-permute-start.3 = (bf16[2,2,3,2,128]{4,3,2,1,0:T(2,128)(2,1)S(1)}, bf16[2,2,3,2,128]{4,3,2,1,0:T(2,128)(2,1)S(1)}, u32[]{:S(2)}, u32[]{:S(2)}) collective-permute-start(bf16[2,2,3,2,128]{4,3,2,1,0:T(2,128)(2,1)S(1)} %pad_maximum_fusion.refs_0_), channel_id=1, source_target_pairs={{0,16},{1,17},{2,18},{3,19},{4,28},{5,29},{6,30},{7,31},{8,24},{9,... | collective-permute-start | bytes 18440 | tf_op jit(solution)/shard_map/ppermute | solution.py:201
  5.7 0.9 %collective-permute-start.2 = (bf16[2,2,3,2,128]{4,3,2,1,0:T(2,128)(2,1)S(1)}, bf16[2,2,3,2,128]{4,3,2,1,0:T(2,128)(2,1)S(1)}, u32[]{:S(2)}, u32[]{:S(2)}) collective-permute-start(bf16[2,2,3,2,128]{4,3,2,1,0:T(2,128)(2,1)S(1)} %pad_maximum_fusion.refs_0_), channel_id=1, source_target_pairs={{0,12},{1,13},{2,14},{3,15},{4,8},{5,9},{6,10},{7,11},{8,4},{9,5},... | collective-permute-start | bytes 18440 | tf_op jit(solution)/shard_map/ppermute | solution.py:201
  6.6 1.3 %collective-permute-done.3.refs_1_ = bf16[2,2,3,2,128]{4,3,2,1,0:T(2,128)(2,1)S(1)} collective-permute-done((bf16[2,2,3,2,128]{4,3,2,1,0:T(2,128)(2,1)S(1)}, bf16[2,2,3,2,128]{4,3,2,1,0:T(2,128)(2,1)S(1)}, u32[]{:S(2)}, u32[]{:S(2)}) %collective-permute-start.3) | collective-permute-done | bytes 6176 | tf_op jit(solution)/shard_map/ppermute | solution.py:201
  7.8 0.0 collective-permute-start.4
  7.9 0.0 collective-permute-done.1.pack_far_ref
  7.9 0.1 %shard_map.65.refs_2_ = f32[64,128]{1,0:T(8,128)S(1)} custom-call(s32[1]{0:T(128)} %bitcast.place_ref, bf16[73,4,128]{2,1,0:T(4,128)(2,1)S(1)} %collective-permute-done.pack_ref, bf16[73,4,128]{2,1,0:T(4,128)(2,1)S(1)} %collective-permute-done.1.pack_far_ref, bf16[2,2,3,2,128]{4,3,2,1,0:T(2,128)(2,1)S(1)} %pad_maximum_fusion.refs_0_, ...), custom_call_target="tpu_custom_call" | custom-call | tf_op jit(solution)/shard_map/pallas_call | solution.py:23
  8.0 0.8 %collective-permute-done.2.refs_0_ = bf16[2,2,3,2,128]{4,3,2,1,0:T(2,128)(2,1)S(1)} collective-permute-done((bf16[2,2,3,2,128]{4,3,2,1,0:T(2,128)(2,1)S(1)}, bf16[2,2,3,2,128]{4,3,2,1,0:T(2,128)(2,1)S(1)}, u32[]{:S(2)}, u32[]{:S(2)}) %collective-permute-start.2) | collective-permute-done | bytes 6176 | tf_op jit(solution)/shard_map/ppermute | solution.py:201
  8.8 0.2 %collective-permute-done.4.refs_1_ = bf16[2,2,3,2,128]{4,3,2,1,0:T(2,128)(2,1)S(1)} collective-permute-done((bf16[2,2,3,2,128]{4,3,2,1,0:T(2,128)(2,1)S(1)}, bf16[2,2,3,2,128]{4,3,2,1,0:T(2,128)(2,1)S(1)}, u32[]{:S(2)}, u32[]{:S(2)}) %collective-permute-start.4) | collective-permute-done | bytes 6176 | tf_op jit(solution)/shard_map/ppermute | solution.py:201
  9.0 0.0 copy-start
  9.0 0.0 copy-start.1
  9.0 0.0 copy-start.2
  9.0 0.2 %shard_map.66 = f32[16,128]{1,0:T(8,128)S(1)} custom-call(s32[1]{0:T(128)} %bitcast.place_ref, bf16[73,4,128]{2,1,0:T(4,128)(2,1)S(1)} %collective-permute-done.pack_ref, bf16[73,4,128]{2,1,0:T(4,128)(2,1)S(1)} %collective-permute-done.1.pack_far_ref, bf16[2,2,3,2,128]{4,3,2,1,0:T(2,128)(2,1)S(1)} %collective-permute-done.2.refs_0_, ...), custom_call_target="tpu_custom_call" | custom-call | tf_op jit(solution)/shard_map/pallas_call | solution.py:23
  9.2 2.7 %collective-permute-start.6 = (f32[16,128]{1,0:T(8,128)S(1)}, f32[16,128]{1,0:T(8,128)S(1)}, u32[]{:S(2)}, u32[]{:S(2)}) collective-permute-start(f32[16,128]{1,0:T(8,128)S(1)} %shard_map.66), channel_id=1, source_target_pairs={{0,6},{1,7},{2,4},{3,5},{4,2},{5,3},{6,0},{7,1},{8,14},{9,15},{10,... | collective-permute-start | bytes 24584 | tf_op jit(solution)/shard_map/ppermute | solution.py:201
  12.0 0.0 collective-permute-start.5
  12.0 0.0 copy-done
  12.0 0.0 copy-done.1
  12.0 0.0 copy-done.2
  12.0 0.6 %shard_map.67 = (f32[16,1024]{1,0:T(8,128)S(1)}, f32[16,1024]{1,0:T(8,128)S(1)}, bf16[256,2048]{1,0:T(8,128)(2,1)S(1)}) custom-call(s32[1]{0:T(128)} %bitcast.8.own_ref, s32[16,256]{1,0:T(8,128)S(1)} %copy-done, s32[16,256]{1,0:T(8,128)S(1)} %copy-done.1, s32[16,256]{1,0:T(8,128)S(1)} %copy-done.2), custom_call_target="tpu_custom_call" | custom-call | tf_op jit(solution)/shard_map/pallas_call | solution.py:23
  12.6 0.8 %collective-permute-done.6 = f32[16,128]{1,0:T(8,128)S(1)} collective-permute-done((f32[16,128]{1,0:T(8,128)S(1)}, f32[16,128]{1,0:T(8,128)S(1)}, u32[]{:S(2)}, u32[]{:S(2)}) %collective-permute-start.6) | collective-permute-done | bytes 8224 | tf_op jit(solution)/shard_map/ppermute | solution.py:201
  13.3 0.0 collective-permute-done.5
  13.3 1.0 %shard_map.68 = f32[16,64]{1,0:T(8,128)} custom-call(f32[1,16,128]{2,1,0:T(8,128)S(1)} %bitcast.10, f32[1,16,128]{2,1,0:T(8,128)S(1)} %bitcast.9, f32[16,1024]{1,0:T(8,128)S(1)} %get-tuple-element.8.cos_ref, f32[16,1024]{1,0:T(8,128)S(1)} %get-tuple-element.9.sin_ref, bf16[256,2048]{1,0:T(8,128)(2,1)S(1)} %get-tuple-element.10.factor_ref), custom_call_target="tpu_custom_call" | custom-call | tf_op jit(solution)/shard_map/pallas_call | solution.py:23
  (3 shorter events, 0.0 us)
Async XLA Ops:
  0.9 3.2 %collective-permute-start = (bf16[73,4,128]{2,1,0:T(4,128)(2,1)S(1)}, bf16[73,4,128]{2,1,0:T(4,128)(2,1)S(1)}, u32[]{:S(2)}, u32[]{:S(2)}) collective-permute-start(bf16[73,4,128]{2,1,0:T(4,128)(2,1)S(1)} %shard_map.64), channel_id=1, source_target_pairs={{0,4},{1,5},{2,6},{3,7},{4,0},{5,1},{6,2},{7,3},{8,12},{9,13},{10,... | collective-permute-start | bytes 224264 | tf_op jit(solution)/shard_map/ppermute | solution.py:201
  1.4 6.4 %collective-permute-start.1 = (bf16[73,4,128]{2,1,0:T(4,128)(2,1)S(1)}, bf16[73,4,128]{2,1,0:T(4,128)(2,1)S(1)}, u32[]{:S(2)}, u32[]{:S(2)}) collective-permute-start(bf16[73,4,128]{2,1,0:T(4,128)(2,1)S(1)} %shard_map.64), channel_id=1, source_target_pairs={{0,5},{1,4},{2,7},{3,6},{4,1},{5,0},{6,3},{7,2},{8,13},{9,12},{10,... | collective-permute-start | bytes 224264 | tf_op jit(solution)/shard_map/ppermute | solution.py:201
  4.1 3.7 %collective-permute-start.3 = (bf16[2,2,3,2,128]{4,3,2,1,0:T(2,128)(2,1)S(1)}, bf16[2,2,3,2,128]{4,3,2,1,0:T(2,128)(2,1)S(1)}, u32[]{:S(2)}, u32[]{:S(2)}) collective-permute-start(bf16[2,2,3,2,128]{4,3,2,1,0:T(2,128)(2,1)S(1)} %pad_maximum_fusion.refs_0_), channel_id=1, source_target_pairs={{0,16},{1,17},{2,18},{3,19},{4,28},{5,29},{6,30},{7,31},{8,24},{9,... | collective-permute-start | bytes 18440 | tf_op jit(solution)/shard_map/ppermute | solution.py:201
  5.7 3.1 %collective-permute-start.2 = (bf16[2,2,3,2,128]{4,3,2,1,0:T(2,128)(2,1)S(1)}, bf16[2,2,3,2,128]{4,3,2,1,0:T(2,128)(2,1)S(1)}, u32[]{:S(2)}, u32[]{:S(2)}) collective-permute-start(bf16[2,2,3,2,128]{4,3,2,1,0:T(2,128)(2,1)S(1)} %pad_maximum_fusion.refs_0_), channel_id=1, source_target_pairs={{0,12},{1,13},{2,14},{3,15},{4,8},{5,9},{6,10},{7,11},{8,4},{9,5},... | collective-permute-start | bytes 18440 | tf_op jit(solution)/shard_map/ppermute | solution.py:201
  7.8 1.2 %collective-permute-start.4 = (bf16[2,2,3,2,128]{4,3,2,1,0:T(2,128)(2,1)S(1)}, bf16[2,2,3,2,128]{4,3,2,1,0:T(2,128)(2,1)S(1)}, u32[]{:S(2)}, u32[]{:S(2)}) collective-permute-start(bf16[2,2,3,2,128]{4,3,2,1,0:T(2,128)(2,1)S(1)} %collective-permute-done.3.refs_1_), channel_id=1, source_target_pairs={{0,4},{1,5},{2,6},{3,7},{4,0},{5,1},{6,2},{7,3},{8,12},{9,13},{10,... | collective-permute-start | bytes 18440 | tf_op jit(solution)/shard_map/ppermute | solution.py:201
  9.0 3.0 %copy-start = (s32[16,256]{1,0:T(8,128)S(1)}, s32[16,256]{1,0:T(8,128)}, u32[]{:S(2)}) copy-start(s32[16,256]{1,0:T(8,128)} %theta_ref.1) | copy-start | bytes 49156
  9.0 3.0 %copy-start.1 = (s32[16,256]{1,0:T(8,128)S(1)}, s32[16,256]{1,0:T(8,128)}, u32[]{:S(2)}) copy-start(s32[16,256]{1,0:T(8,128)} %phi_ref.1) | copy-start | bytes 49156
  9.0 3.0 %copy-start.2 = (s32[16,256]{1,0:T(8,128)S(1)}, s32[16,256]{1,0:T(8,128)}, u32[]{:S(2)}) copy-start(s32[16,256]{1,0:T(8,128)} %psi_ref.1) | copy-start | bytes 49156
  9.2 4.1 %collective-permute-start.6 = (f32[16,128]{1,0:T(8,128)S(1)}, f32[16,128]{1,0:T(8,128)S(1)}, u32[]{:S(2)}, u32[]{:S(2)}) collective-permute-start(f32[16,128]{1,0:T(8,128)S(1)} %shard_map.66), channel_id=1, source_target_pairs={{0,6},{1,7},{2,4},{3,5},{4,2},{5,3},{6,0},{7,1},{8,14},{9,15},{10,... | collective-permute-start | bytes 24584 | tf_op jit(solution)/shard_map/ppermute | solution.py:201
  12.0 1.4 %collective-permute-start.5 = (f32[16,128]{1,0:T(8,128)S(1)}, f32[16,128]{1,0:T(8,128)S(1)}, u32[]{:S(2)}, u32[]{:S(2)}) collective-permute-start(f32[16,128]{1,0:T(8,128)S(1)} %shard_map.66), channel_id=1, source_target_pairs={{0,4},{1,5},{2,6},{3,7},{4,0},{5,1},{6,2},{7,3},{8,12},{9,13},{10,... | collective-permute-start | bytes 24584 | tf_op jit(solution)/shard_map/ppermute | solution.py:201

commit v5 on v4

--- a/solution.py
+++ b/solution.py
@@ -31,17 +31,10 @@
     )(*args)
 
 
-def staged(*refs):
-    *given, out_ref, sems = refs
-    copies, start = [], 0
-    for i, ref in enumerate(given):
-        stop = start + ref.shape[0]
-        copies.append(pltpu.make_async_copy(ref, out_ref.at[start:stop], sems.at[i]))
-        start = stop
-    for copy in copies:
-        copy.start()
-    for copy in copies:
-        copy.wait()
+def joined(near_ref, far_ref, out_ref):
+    rows = near_ref.shape[0]
+    out_ref[:rows] = near_ref[...]
+    out_ref[rows:] = far_ref[...]
 
 
 def cos_sin(steps, period):
@@ -71,7 +64,12 @@
     return held
 
 
-def features(cycles, planes, width, own_ref, theta_ref, phi_ref, psi_ref, cos_ref, sin_ref, factor_ref):
+def plane_rows(planes, own_ref, out_ref):
+    row = lax.broadcasted_iota(jnp.int32, out_ref.shape, 0)
+    out_ref[...] = (own_ref[0] ^ (row // planes)) * planes + row % planes
+
+
+def features(cycles, planes, width, own_ref, theta_ref, phi_ref, psi_ref, plane_ref, cos_ref, sin_ref, factor_ref):
     own = own_ref[0]
     modes = cos_ref.shape[0]
     wide = 2 * planes
@@ -95,9 +93,7 @@
         chosen = [theta == cycle for cycle in range(cycles)]
         firsts, seconds = [], []
         for half in range(halves):
-            inner = lax.broadcasted_iota(jnp.int32, (wide, LANES), 0)
-            part = (own ^ (2 * half)) ^ (inner // planes)
-            plane = part * planes + inner % planes
+            plane = plane_ref[half * wide : (half + 1) * wide, :]
             c, s = cos_sin((plane * psi) & (NPSI - 1), NPSI)
             for pick in chosen:
                 c_own, s_own = jnp.where(pick, c, 0.0), jnp.where(pick, s, 0.0)
@@ -110,25 +106,25 @@
             factor_ref[:, pl.ds((2 * row + i) * LANES, LANES)] = jnp.concatenate([high, low], axis=0)
 
 
-def cubes(masks, shape, sources, place_ref, pack_ref, pack_far_ref, *refs):
-    cycles, modes, planes = shape
+def cubes(masks, sources, place_ref, table_ref, table_far_ref, beam_ref, beam_far_ref, *refs):
     *refs, out_ref = refs
+    cycles, modes, planes, _ = table_ref.shape
     place = place_ref[0]
     blocks, kinds, each = refs[0].shape[0], refs[0].shape[2], refs[0].shape[3]
     rows, width = 2 * cycles * 2 * planes, max(modes, LANES)
     f32 = jnp.float32
     lane = lax.broadcasted_iota(jnp.int32, (rows, width), 1)
 
-    def both(row):
-        return jnp.concatenate([pack_ref[row], pack_far_ref[row]], axis=0).astype(f32)
-
-    beam = [[both(cycles * modes + k * kinds + c) for c in range(kinds)] for k in range(2)]
+    def both(near_ref, far_ref, *at):
+        return jnp.concatenate([near_ref[at], far_ref[at]], axis=0).astype(f32)
+
+    beam = [[both(beam_ref, beam_far_ref, k, c) for c in range(kinds)] for k in range(2)]
 
     def one_mode(mode, sky, total):
         real = sum(sky[0][c] * beam[0][c] - sky[1][c] * beam[1][c] for c in range(kinds))
         imag = sum(sky[0][c] * beam[1][c] + sky[1][c] * beam[0][c] for c in range(kinds))
         spectra = [v.astype(jnp.bfloat16).astype(f32) for v in (real, imag)]
-        tables = [both(g * modes + mode) for g in range(cycles)]
+        tables = [both(table_ref, table_far_ref, g, mode) for g in range(cycles)]
         products = jnp.concatenate([s * t for t in tables for s in spectra], axis=0)
         return jnp.where(lane == mode, jnp.sum(products, axis=1, keepdims=True), total)
 
@@ -190,9 +186,6 @@
     width = theta_index.shape[1] // parts
     samples = detectors * width
 
-    def in_hbm(values):
-        return pltpu.with_memory_space_constraint(values, pltpu.HBM)
-
     def trade(values, det_mask, bm_mask=0, odd_mask=None):
         pairs = []
         for i in range(groups):
@@ -200,23 +193,19 @@
             pairs += [(i * parts + j, (i ^ mask) * parts + (j ^ bm_mask)) for j in range(parts)]
         return lax.ppermute(values, ("det", "bm"), pairs)
 
-    given = [values.reshape((-1,) + wigner.shape[2:]) for values in (wigner, beam_blm, sky_alm)]
-    length = sum(values.shape[0] for values in given)
-    pack = pl.pallas_call(
-        staged,
-        out_shape=jax.ShapeDtypeStruct((length,) + wigner.shape[2:], bf16),
-        in_specs=[pl.BlockSpec(memory_space=pltpu.HBM)] * 3,
-        out_specs=pl.BlockSpec(memory_space=pltpu.VMEM),
-        scratch_shapes=[pltpu.SemaphoreType.DMA((3,))],
-        compiler_params=pltpu.CompilerParams(vmem_limit_bytes=16 << 20),
-    )(*[in_hbm(values) for values in given])
-
-    def sky_of(values):
-        return values[length - given[2].shape[0] :].reshape((1,) + sky_alm.shape)
-
-    pack_near = trade(pack, 1)
-    pack_far = trade(pack, 1, 1)
-    held = jnp.concatenate([sky_of(pack), sky_of(pack_near)])
+    sky_near = trade(sky_alm[None], 1)
+    table_far = trade(wigner, 1, 1)
+    beam_far = trade(beam_blm, 1, 1)
+    table_near = trade(wigner, 1)
+    plane_ids = kernel_call(
+        functools.partial(plane_rows, planes),
+        jax.ShapeDtypeStruct((parts * planes, LANES), jnp.int32),
+        own.reshape(1),
+        flops=10_000_000,
+    )
+    held = kernel_call(
+        joined, jax.ShapeDtypeStruct((2,) + sky_alm.shape, bf16), sky_alm[None], sky_near, scalars=0
+    )
     masks = [(1 << level) | 1 for level in range(3, groups.bit_length() - 1)]
     for mask in masks:
         held = jnp.concatenate([held, trade(held, mask)])
@@ -234,12 +223,12 @@
         theta_index,
         phi_index,
         psi_index,
+        plane_ids,
     )
 
     def half_cube(outs, sources, *skies):
-        return kernel_call(
-            functools.partial(cubes, masks, (cycles, modes, planes), sources), outs, place.reshape(1), pack_near, pack_far, *skies
-        )
+        tables = (table_near, table_far, beam_blm, beam_far)
+        return kernel_call(functools.partial(cubes, masks, sources), outs, place.reshape(1), *tables, *skies)
 
     columns = jax.ShapeDtypeStruct((rows, max(modes, LANES)), f32)
     half = half_cube(columns, ((0, 0), (4, 6)), held, sky_a)

time: 14.5 us -> 16.1 us (1.11)
  local copies, waits for them, and re-layouts: 0.02 us -> 1.4 us
  Pallas kernels: 2.77 us -> 1.91 us
  starting transfers between devices: 8.43 us -> 9.09 us
  waiting for transfers between devices: 3.03 us -> 3.48 us
    unnamed x6 -> x10, local copies, waits for them, and re-layouts: 0.01 us -> 1.4 us
    pallas_call x1 -> x0, Pallas kernels: 0.87 us -> none  [on_device(): pl.pallas_call(staged, out_shape=jax.ShapeDtypeStruct((length,) + wigner....]
    ppermute x7 -> x9, starting transfers between devices: 8.43 us -> 9.09 us  [trade(): return lax.ppermute(values, ('det', 'bm'), pairs)]
    ppermute x7 -> x9, waiting for transfers between devices: 3.03 us -> 3.48 us  [trade(): return lax.ppermute(values, ('det', 'bm'), pairs)]
    pallas_call x4 -> x6, Pallas kernels: 1.9 us -> 1.91 us  [kernel_call(): pl.pallas_call(body, out_shape=outs, in_specs=[pl.BlockSpec(memory_space=...]
  transfers between devices with their start and end apart: 7 -> 9, of which waited for: 4 -> 4; matrix products, arithmetic and copies ran while one was open for 0% -> 0% of each run, Pallas kernels for 5% -> 5%
where the time goes in v5:
time: 16.1 us; the launch traced here: 15.9 us
  starting transfers between devices  9.09 us (56%)
  waiting for transfers between devices  3.48 us (22%)
  Pallas kernels  1.91 us (12%)
  local copies, waits for them, and re-layouts  1.4 us (9%)
    ppermute x9, starting transfers between devices, trade(): return lax.ppermute(values, ('det', 'bm'), pairs)  9.09 us
    ppermute x9, waiting for transfers between devices, trade(): return lax.ppermute(values, ('det', 'bm'), pairs)  3.48 us
    pallas_call x6, Pallas kernels, kernel_call(): pl.pallas_call(body, out_shape=outs, in_specs=[pl.BlockSpec(memory_space=...  1.91 us
    unnamed x10, local copies, waits for them, and re-layouts  1.4 us
  transfers between devices with their start and end apart: 9, of which 4 were waited for; matrix products, arithmetic and copies ran while one was open for 0% of the time, Pallas kernels for 5%

profile of v5, /device:TPU:0, one launch (start us, length us, event | category | flops | bytes accessed | tf_op | source)
XLA Modules:
  0.0 15.9 jit_solution(9903084178944947984)
XLA Ops:
  0.0 2.5 %collective-permute-start.1 = (bf16[4,16,4,128]{3,2,1,0:T(4,128)(2,1)}, bf16[4,16,4,128]{3,2,1,0:T(4,128)(2,1)S(1)}, u32[]{:S(2)}, u32[]{:S(2)}) collective-permute-start(bf16[4,16,4,128]{3,2,1,0:T(4,128)(2,1)} %param.8), channel_id=1, source_target_pairs={{0,5},{1,4},{2,7},{3,6},{4,1},{5,0},{6,3},{7,2},{8,13},{9,12},{10,... | collective-permute-start | bytes 196616 | tf_op jit(solution)/shard_map/ppermute | solution.py:194
  2.5 0.7 %collective-permute-start = (bf16[4,16,4,128]{3,2,1,0:T(4,128)(2,1)}, bf16[4,16,4,128]{3,2,1,0:T(4,128)(2,1)S(1)}, u32[]{:S(2)}, u32[]{:S(2)}) collective-permute-start(bf16[4,16,4,128]{3,2,1,0:T(4,128)(2,1)} %param.8), channel_id=1, source_target_pairs={{0,4},{1,5},{2,6},{3,7},{4,0},{5,1},{6,2},{7,3},{8,12},{9,13},{10,... | collective-permute-start | bytes 196616 | tf_op jit(solution)/shard_map/ppermute | solution.py:194
  3.2 0.0 copy-start
  3.2 0.0 collective-permute-start.3
  3.2 1.4 %collective-permute-done.3.far_ref = bf16[1,2,3,2,128]{4,3,2,1,0:T(2,128)(2,1)S(1)} collective-permute-done((bf16[1,2,3,2,128]{4,3,2,1,0:T(2,128)(2,1)}, bf16[1,2,3,2,128]{4,3,2,1,0:T(2,128)(2,1)S(1)}, u32[]{:S(2)}, u32[]{:S(2)}) %collective-permute-start.3) | collective-permute-done | bytes 3104 | tf_op jit(solution)/shard_map/ppermute | solution.py:194
  4.5 0.0 copy-start.4
  4.5 0.7 %copy-done.4 = bf16[2,3,2,128]{3,2,1,0:T(2,128)(2,1)S(1)} copy-done((bf16[2,3,2,128]{3,2,1,0:T(2,128)(2,1)S(1)}, bf16[2,3,2,128]{3,2,1,0:T(2,128)(2,1)}, u32[]{:S(2)}) %copy-start.4) | copy-done | bytes 3096
  5.2 1.5 %collective-permute-start.5 = (bf16[2,2,3,2,128]{4,3,2,1,0:T(2,128)(2,1)S(1)}, bf16[2,2,3,2,128]{4,3,2,1,0:T(2,128)(2,1)S(1)}, u32[]{:S(2)}, u32[]{:S(2)}) collective-permute-start(bf16[2,2,3,2,128]{4,3,2,1,0:T(2,128)(2,1)S(1)} %shard_map.64.refs_0_), channel_id=1, source_target_pairs={{0,16},{1,17},{2,18},{3,19},{4,28},{5,29},{6,30},{7,31},{8,24},{9,... | collective-permute-start | bytes 18440 | tf_op jit(solution)/shard_map/ppermute | solution.py:194
  6.8 0.0 copy-done
  6.8 0.9 %collective-permute-start.2 = (bf16[2,3,4,128]{3,2,1,0:T(4,128)(2,1)S(1)}, bf16[2,3,4,128]{3,2,1,0:T(4,128)(2,1)S(1)}, u32[]{:S(2)}, u32[]{:S(2)}) collective-permute-start(bf16[2,3,4,128]{3,2,1,0:T(4,128)(2,1)S(1)} %copy-done), channel_id=1, source_target_pairs={{0,5},{1,4},{2,7},{3,6},{4,1},{5,0},{6,3},{7,2},{8,13},{9,12},{10,... | collective-permute-start | bytes 18440 | tf_op jit(solution)/shard_map/ppermute | solution.py:194
  7.6 0.8 %collective-permute-start.4 = (bf16[2,2,3,2,128]{4,3,2,1,0:T(2,128)(2,1)S(1)}, bf16[2,2,3,2,128]{4,3,2,1,0:T(2,128)(2,1)S(1)}, u32[]{:S(2)}, u32[]{:S(2)}) collective-permute-start(bf16[2,2,3,2,128]{4,3,2,1,0:T(2,128)(2,1)S(1)} %shard_map.64.refs_0_), channel_id=1, source_target_pairs={{0,12},{1,13},{2,14},{3,15},{4,8},{5,9},{6,10},{7,11},{8,4},{9,5},... | collective-permute-start | bytes 18440 | tf_op jit(solution)/shard_map/ppermute | solution.py:194
  8.4 0.4 %collective-permute-done.5.refs_1_ = bf16[2,2,3,2,128]{4,3,2,1,0:T(2,128)(2,1)S(1)} collective-permute-done((bf16[2,2,3,2,128]{4,3,2,1,0:T(2,128)(2,1)S(1)}, bf16[2,2,3,2,128]{4,3,2,1,0:T(2,128)(2,1)S(1)}, u32[]{:S(2)}, u32[]{:S(2)}) %collective-permute-start.5) | collective-permute-done | bytes 6176 | tf_op jit(solution)/shard_map/ppermute | solution.py:194
  8.9 0.0 collective-permute-start.6
  8.9 0.9 %collective-permute-done.2.beam_far_ref = bf16[2,3,4,128]{3,2,1,0:T(4,128)(2,1)S(1)} collective-permute-done((bf16[2,3,4,128]{3,2,1,0:T(4,128)(2,1)S(1)}, bf16[2,3,4,128]{3,2,1,0:T(4,128)(2,1)S(1)}, u32[]{:S(2)}, u32[]{:S(2)}) %collective-permute-start.2) | collective-permute-done | bytes 6176 | tf_op jit(solution)/shard_map/ppermute | solution.py:194
  9.8 0.0 collective-permute-done.1.table_far_ref
  9.8 0.0 collective-permute-done.table_ref
  9.8 0.1 shard_map.65.refs_2_
  10.0 0.7 %collective-permute-done.4.refs_0_ = bf16[2,2,3,2,128]{4,3,2,1,0:T(2,128)(2,1)S(1)} collective-permute-done((bf16[2,2,3,2,128]{4,3,2,1,0:T(2,128)(2,1)S(1)}, bf16[2,2,3,2,128]{4,3,2,1,0:T(2,128)(2,1)S(1)}, u32[]{:S(2)}, u32[]{:S(2)}) %collective-permute-start.4) | collective-permute-done | bytes 6176 | tf_op jit(solution)/shard_map/ppermute | solution.py:194
  10.7 0.0 collective-permute-done.6.refs_1_
  10.7 0.0 copy-start.3
  10.7 0.2 %shard_map.66 = f32[16,128]{1,0:T(8,128)S(1)} custom-call(s32[1]{0:T(128)} %bitcast.place_ref, bf16[4,16,4,128]{3,2,1,0:T(4,128)(2,1)S(1)} %collective-permute-done.table_ref, bf16[4,16,4,128]{3,2,1,0:T(4,128)(2,1)S(1)} %collective-permute-done.1.table_far_ref, bf16[2,3,4,128]{3,2,1,0:T(4,128)(2,1)S(1)} %copy-done, ...), custom_call_target="tpu_custom_call" | custom-call | tf_op jit(solution)/shard_map/pallas_call | solution.py:23
  10.9 2.5 %collective-permute-start.8 = (f32[16,128]{1,0:T(8,128)S(1)}, f32[16,128]{1,0:T(8,128)S(1)}, u32[]{:S(2)}, u32[]{:S(2)}) collective-permute-start(f32[16,128]{1,0:T(8,128)S(1)} %shard_map.66), channel_id=1, source_target_pairs={{0,6},{1,7},{2,4},{3,5},{4,2},{5,3},{6,0},{7,1},{8,14},{9,15},{10,... | collective-permute-start | bytes 24584 | tf_op jit(solution)/shard_map/ppermute | solution.py:194
  13.4 0.2 %collective-permute-start.7 = (f32[16,128]{1,0:T(8,128)S(1)}, f32[16,128]{1,0:T(8,128)S(1)}, u32[]{:S(2)}, u32[]{:S(2)}) collective-permute-start(f32[16,128]{1,0:T(8,128)S(1)} %shard_map.66), channel_id=1, source_target_pairs={{0,4},{1,5},{2,6},{3,7},{4,0},{5,1},{6,2},{7,3},{8,12},{9,13},{10,... | collective-permute-start | bytes 24584 | tf_op jit(solution)/shard_map/ppermute | solution.py:194
  13.6 0.0 copy-start.1
  13.6 0.0 copy-start.2
  13.7 0.0 copy-done.3
  13.7 0.7 %copy-done.1 = s32[16,256]{1,0:T(8,128)S(1)} copy-done((s32[16,256]{1,0:T(8,128)S(1)}, s32[16,256]{1,0:T(8,128)}, u32[]{:S(2)}) %copy-start.1) | copy-done | bytes 16408
  14.4 0.0 copy-done.2
  14.4 0.6 %shard_map.68 = (f32[16,1024]{1,0:T(8,128)S(1)}, f32[16,1024]{1,0:T(8,128)S(1)}, bf16[256,2048]{1,0:T(8,128)(2,1)S(1)}) custom-call(s32[1]{0:T(128)} %bitcast.4.own_ref, s32[16,256]{1,0:T(8,128)S(1)} %copy-done.1, s32[16,256]{1,0:T(8,128)S(1)} %copy-done.2, s32[16,256]{1,0:T(8,128)S(1)} %copy-done.3, s32[16,128]{1,0:T(8,128)S(1)} %shard_map.67.plane_ref), custom_call_target="tpu_custom_call" | custom-call | tf_op jit(solution)/shard_map/pallas_call | solution.py:23
  15.0 0.0 collective-permute-done.8
  15.0 0.0 collective-permute-done.7
  15.0 1.0 %shard_map.69 = f32[16,64]{1,0:T(8,128)} custom-call(f32[1,16,128]{2,1,0:T(8,128)S(1)} %bitcast.6, f32[1,16,128]{2,1,0:T(8,128)S(1)} %bitcast.5, f32[16,1024]{1,0:T(8,128)S(1)} %get-tuple-element.8.cos_ref, f32[16,1024]{1,0:T(8,128)S(1)} %get-tuple-element.9.sin_ref, bf16[256,2048]{1,0:T(8,128)(2,1)S(1)} %get-tuple-element.10.factor_ref), custom_call_target="tpu_custom_call" | custom-call | tf_op jit(solution)/shard_map/pallas_call | solution.py:23
  (2 shorter events, 0.0 us)
Async XLA Ops:
  0.0 9.8 %collective-permute-start.1 = (bf16[4,16,4,128]{3,2,1,0:T(4,128)(2,1)}, bf16[4,16,4,128]{3,2,1,0:T(4,128)(2,1)S(1)}, u32[]{:S(2)}, u32[]{:S(2)}) collective-permute-start(bf16[4,16,4,128]{3,2,1,0:T(4,128)(2,1)} %param.8), channel_id=1, source_target_pairs={{0,5},{1,4},{2,7},{3,6},{4,1},{5,0},{6,3},{7,2},{8,13},{9,12},{10,... | collective-permute-start | bytes 196616 | tf_op jit(solution)/shard_map/ppermute | solution.py:194
  2.5 7.3 %collective-permute-start = (bf16[4,16,4,128]{3,2,1,0:T(4,128)(2,1)}, bf16[4,16,4,128]{3,2,1,0:T(4,128)(2,1)S(1)}, u32[]{:S(2)}, u32[]{:S(2)}) collective-permute-start(bf16[4,16,4,128]{3,2,1,0:T(4,128)(2,1)} %param.8), channel_id=1, source_target_pairs={{0,4},{1,5},{2,6},{3,7},{4,0},{5,1},{6,2},{7,3},{8,12},{9,13},{10,... | collective-permute-start | bytes 196616 | tf_op jit(solution)/shard_map/ppermute | solution.py:194
  3.2 3.6 %copy-start = (bf16[2,3,4,128]{3,2,1,0:T(4,128)(2,1)S(1)}, bf16[2,3,4,128]{3,2,1,0:T(4,128)(2,1)}, u32[]{:S(2)}) copy-start(bf16[2,3,4,128]{3,2,1,0:T(4,128)(2,1)} %beam_ref.3) | copy-start | bytes 18436
  3.2 1.4 %collective-permute-start.3 = (bf16[1,2,3,2,128]{4,3,2,1,0:T(2,128)(2,1)}, bf16[1,2,3,2,128]{4,3,2,1,0:T(2,128)(2,1)S(1)}, u32[]{:S(2)}, u32[]{:S(2)}) collective-permute-start(bf16[1,2,3,2,128]{4,3,2,1,0:T(2,128)(2,1)} %bitcast.7), channel_id=1, source_target_pairs={{0,4},{1,5},{2,6},{3,7},{4,0},{5,1},{6,2},{7,3},{8,12},{9,13},{10,... | collective-permute-start | bytes 9224 | tf_op jit(solution)/shard_map/ppermute | solution.py:194
  4.5 0.7 %copy-start.4 = (bf16[2,3,2,128]{3,2,1,0:T(2,128)(2,1)S(1)}, bf16[2,3,2,128]{3,2,1,0:T(2,128)(2,1)}, u32[]{:S(2)}) copy-start(bf16[2,3,2,128]{3,2,1,0:T(2,128)(2,1)} %param.6) | copy-start | bytes 9220
  5.2 3.6 %collective-permute-start.5 = (bf16[2,2,3,2,128]{4,3,2,1,0:T(2,128)(2,1)S(1)}, bf16[2,2,3,2,128]{4,3,2,1,0:T(2,128)(2,1)S(1)}, u32[]{:S(2)}, u32[]{:S(2)}) collective-permute-start(bf16[2,2,3,2,128]{4,3,2,1,0:T(2,128)(2,1)S(1)} %shard_map.64.refs_0_), channel_id=1, source_target_pairs={{0,16},{1,17},{2,18},{3,19},{4,28},{5,29},{6,30},{7,31},{8,24},{9,... | collective-permute-start | bytes 18440 | tf_op jit(solution)/shard_map/ppermute | solution.py:194
  6.8 3.1 %collective-permute-start.2 = (bf16[2,3,4,128]{3,2,1,0:T(4,128)(2,1)S(1)}, bf16[2,3,4,128]{3,2,1,0:T(4,128)(2,1)S(1)}, u32[]{:S(2)}, u32[]{:S(2)}) collective-permute-start(bf16[2,3,4,128]{3,2,1,0:T(4,128)(2,1)S(1)} %copy-done), channel_id=1, source_target_pairs={{0,5},{1,4},{2,7},{3,6},{4,1},{5,0},{6,3},{7,2},{8,13},{9,12},{10,... | collective-permute-start | bytes 18440 | tf_op jit(solution)/shard_map/ppermute | solution.py:194
  7.6 3.1 %collective-permute-start.4 = (bf16[2,2,3,2,128]{4,3,2,1,0:T(2,128)(2,1)S(1)}, bf16[2,2,3,2,128]{4,3,2,1,0:T(2,128)(2,1)S(1)}, u32[]{:S(2)}, u32[]{:S(2)}) collective-permute-start(bf16[2,2,3,2,128]{4,3,2,1,0:T(2,128)(2,1)S(1)} %shard_map.64.refs_0_), channel_id=1, source_target_pairs={{0,12},{1,13},{2,14},{3,15},{4,8},{5,9},{6,10},{7,11},{8,4},{9,5},... | collective-permute-start | bytes 18440 | tf_op jit(solution)/shard_map/ppermute | solution.py:194
  8.9 1.8 %collective-permute-start.6 = (bf16[2,2,3,2,128]{4,3,2,1,0:T(2,128)(2,1)S(1)}, bf16[2,2,3,2,128]{4,3,2,1,0:T(2,128)(2,1)S(1)}, u32[]{:S(2)}, u32[]{:S(2)}) collective-permute-start(bf16[2,2,3,2,128]{4,3,2,1,0:T(2,128)(2,1)S(1)} %collective-permute-done.5.refs_1_), channel_id=1, source_target_pairs={{0,4},{1,5},{2,6},{3,7},{4,0},{5,1},{6,2},{7,3},{8,12},{9,13},{10,... | collective-permute-start | bytes 18440 | tf_op jit(solution)/shard_map/ppermute | solution.py:194
  10.7 3.0 %copy-start.3 = (s32[16,256]{1,0:T(8,128)S(1)}, s32[16,256]{1,0:T(8,128)}, u32[]{:S(2)}) copy-start(s32[16,256]{1,0:T(8,128)} %psi_ref.1) | copy-start | bytes 49156
  10.9 4.1 %collective-permute-start.8 = (f32[16,128]{1,0:T(8,128)S(1)}, f32[16,128]{1,0:T(8,128)S(1)}, u32[]{:S(2)}, u32[]{:S(2)}) collective-permute-start(f32[16,128]{1,0:T(8,128)S(1)} %shard_map.66), channel_id=1, source_target_pairs={{0,6},{1,7},{2,4},{3,5},{4,2},{5,3},{6,0},{7,1},{8,14},{9,15},{10,... | collective-permute-start | bytes 24584 | tf_op jit(solution)/shard_map/ppermute | solution.py:194
  13.4 1.5 %collective-permute-start.7 = (f32[16,128]{1,0:T(8,128)S(1)}, f32[16,128]{1,0:T(8,128)S(1)}, u32[]{:S(2)}, u32[]{:S(2)}) collective-permute-start(f32[16,128]{1,0:T(8,128)S(1)} %shard_map.66), channel_id=1, source_target_pairs={{0,4},{1,5},{2,6},{3,7},{4,0},{5,1},{6,2},{7,3},{8,12},{9,13},{10,... | collective-permute-start | bytes 24584 | tf_op jit(solution)/shard_map/ppermute | solution.py:194
  13.6 0.7 %copy-start.1 = (s32[16,256]{1,0:T(8,128)S(1)}, s32[16,256]{1,0:T(8,128)}, u32[]{:S(2)}) copy-start(s32[16,256]{1,0:T(8,128)} %theta_ref.1) | copy-start | bytes 49156
  13.6 0.7 %copy-start.2 = (s32[16,256]{1,0:T(8,128)S(1)}, s32[16,256]{1,0:T(8,128)}, u32[]{:S(2)}) copy-start(s32[16,256]{1,0:T(8,128)} %phi_ref.1) | copy-start | bytes 49156

commit v6 on v5

--- a/solution.py
+++ b/solution.py
@@ -91,19 +91,16 @@
         else:
             pl.loop(0, modes, step=step)(turn_phi)
         chosen = [theta == cycle for cycle in range(cycles)]
-        firsts, seconds = [], []
+        rows = []
         for half in range(halves):
             plane = plane_ref[half * wide : (half + 1) * wide, :]
             c, s = cos_sin((plane * psi) & (NPSI - 1), NPSI)
             for pick in chosen:
-                c_own, s_own = jnp.where(pick, c, 0.0), jnp.where(pick, s, 0.0)
-                firsts += [c_own, -s_own]
-                seconds += [s_own, c_own]
-        for i, rows in enumerate((firsts, seconds)):
-            full = jnp.concatenate(rows, axis=0)
-            high = full.astype(jnp.bfloat16)
-            low = (full - high.astype(jnp.float32)).astype(jnp.bfloat16)
-            factor_ref[:, pl.ds((2 * row + i) * LANES, LANES)] = jnp.concatenate([high, low], axis=0)
+                rows += [jnp.where(pick, c, 0.0), jnp.where(pick, -s, 0.0)]
+        full = jnp.concatenate(rows, axis=0)
+        high = full.astype(jnp.bfloat16)
+        low = (full - high.astype(jnp.float32)).astype(jnp.bfloat16)
+        factor_ref[:, at] = jnp.concatenate([high, low], axis=0)
 
 
 def cubes(masks, sources, place_ref, table_ref, table_far_ref, beam_ref, beam_far_ref, *refs):
@@ -154,27 +151,33 @@
         out_ref[...] = total
 
 
-def sampled(near_ref, far_ref, cos_ref, sin_ref, factor_ref, out_ref):
-    width = out_ref.shape[1]
+def sampled(planes, near_ref, far_ref, cos_ref, sin_ref, factor_ref, *out_refs):
     halves = [ref[half] for ref in (near_ref, far_ref) for half in range(ref.shape[0])]
     modes, doubled = halves[0].shape
+    wide = 2 * planes
     lane = lax.broadcasted_iota(jnp.int32, (modes, doubled), 1)
     whole = [jnp.where(lane < doubled // 2, *halves[i : i + 2]) for i in range(0, len(halves), 2)]
-    high = [v.astype(jnp.bfloat16) for v in whole]
-    low = [(v - h.astype(jnp.float32)).astype(jnp.bfloat16) for v, h in zip(whole, high)]
-    left = jnp.concatenate(
-        [jnp.concatenate(high + high, axis=1), jnp.concatenate(low + [jnp.zeros_like(v) for v in low], axis=1)], axis=0
-    )
+    is_real = (lane // wide) % 2 == 0
+    turned = [jnp.where(is_real, pltpu.roll(v, doubled - wide, 1), -pltpu.roll(v, wide, 1)) for v in whole]
+    left = []
+    for parts in (whole, turned):
+        high = [v.astype(jnp.bfloat16) for v in parts]
+        low = [(v - h.astype(jnp.float32)).astype(jnp.bfloat16) for v, h in zip(parts, high)]
+        left += [jnp.concatenate(high + high, axis=1)]
+        left += [jnp.concatenate(low + [jnp.zeros_like(v) for v in low], axis=1)]
+    left = jnp.concatenate(left, axis=0)
+    count = factor_ref.shape[1]
+    step = math.gcd(count, 2 * LANES)
     done = []
-    for row in range(out_ref.shape[0] * width // LANES):
-        at = pl.ds(row * LANES, LANES)
-        both = jnp.dot(left, factor_ref[:, pl.ds(2 * row * LANES, 2 * LANES)], preferred_element_type=jnp.float32)
-        both = both[:modes] + both[modes:]
-        done.append(jnp.sum(both[:, :LANES] * cos_ref[:, at] - both[:, LANES:] * sin_ref[:, at], axis=0, keepdims=True))
+    for start in range(0, count, step):
+        at = pl.ds(start, step)
+        both = jnp.dot(left, factor_ref[:, at], preferred_element_type=jnp.float32)
+        real, imag = (both[i : i + modes] + both[i + modes : i + 2 * modes] for i in (0, 2 * modes))
+        total = jnp.sum(real * cos_ref[:, at] - imag * sin_ref[:, at], axis=0, keepdims=True)
+        done += [total[:, i : i + LANES] for i in range(0, step, LANES)]
     result = jnp.concatenate(done, axis=0)
-    rows = result.shape[0]
-    for part in range(LANES // width):
-        out_ref[part * rows : (part + 1) * rows, :] = result[:, part * width : (part + 1) * width]
+    for part, out_ref in enumerate(out_refs):
+        out_ref[...] = result[:, part * out_ref.shape[1] : (part + 1) * out_ref.shape[1]]
 
 
 def on_device(sky_alm, beam_blm, wigner, theta_index, phi_index, psi_index):
@@ -214,7 +217,7 @@
     sky_c = trade(sky_a, 1)
 
     rows = 2 * cycles * 2 * planes
-    factors = jax.ShapeDtypeStruct((2 * parts // 2 * rows, 2 * samples), bf16)
+    factors = jax.ShapeDtypeStruct((2 * parts // 2 * rows, samples), bf16)
     waves = jax.ShapeDtypeStruct((modes, samples), f32)
     factors_of = kernel_call(
         functools.partial(features, cycles, planes, width),
@@ -239,14 +242,15 @@
     while bit < parts:
         far = jnp.concatenate([far, trade(jnp.concatenate([near, far]), 0, bit)])
         bit *= 2
-    return kernel_call(
-        sampled,
-        jax.ShapeDtypeStruct((detectors, width), f32),
+    result = kernel_call(
+        functools.partial(sampled, planes),
+        [jax.ShapeDtypeStruct((samples // LANES, width), f32)] * (LANES // width),
         near,
         far,
         *factors_of,
         scalars=0,
     )
+    return jnp.concatenate(result)
 
 
 def solution(mesh):

time: 16.1 us -> 16 us (level)
  Pallas kernels: 1.91 us -> 1.14 us
  other arithmetic: 0 us -> 0.61 us
    pallas_call x6, Pallas kernels: 1.91 us -> 1.14 us  [kernel_call(): pl.pallas_call(body, out_shape=outs, in_specs=[pl.BlockSpec(memory_space=...]
    concatenate x0 -> x1, other arithmetic: none -> 0.61 us  [on_device(): return jnp.concatenate(result)]
  transfers between devices with their start and end apart: 9 -> 9, of which waited for: 4 -> 5; matrix products, arithmetic and copies ran while one was open for 0% -> 0% of each run, Pallas kernels for 5% -> 4%
where the time goes in v6:
time: 16 us; the launch traced here: 15.8 us
  starting transfers between devices  9.09 us (57%)
  waiting for transfers between devices  3.55 us (22%)
  local copies, waits for them, and re-layouts  1.4 us (9%)
  Pallas kernels  1.14 us (7%)
  other arithmetic  0.61 us (4%)
    ppermute x9, starting transfers between devices, trade(): return lax.ppermute(values, ('det', 'bm'), pairs)  9.09 us
    ppermute x9, waiting for transfers between devices, trade(): return lax.ppermute(values, ('det', 'bm'), pairs)  3.55 us
    unnamed x10, local copies, waits for them, and re-layouts  1.4 us
    pallas_call x6, Pallas kernels, kernel_call(): pl.pallas_call(body, out_shape=outs, in_specs=[pl.BlockSpec(memory_space=...  1.14 us
    concatenate x1, other arithmetic, on_device(): return jnp.concatenate(result)  0.61 us
  transfers between devices with their start and end apart: 9, of which 5 were waited for; matrix products, arithmetic and copies ran while one was open for 0% of the time, Pallas kernels for 4%

profile of v6, /device:TPU:0, one launch (start us, length us, event | category | flops | bytes accessed | tf_op | source)
XLA Modules:
  0.0 15.8 jit_solution(10111064079085811118)
XLA Ops:
  0.0 2.5 %collective-permute-start.1 = (bf16[4,16,4,128]{3,2,1,0:T(4,128)(2,1)}, bf16[4,16,4,128]{3,2,1,0:T(4,128)(2,1)S(1)}, u32[]{:S(2)}, u32[]{:S(2)}) collective-permute-start(bf16[4,16,4,128]{3,2,1,0:T(4,128)(2,1)} %param.8), channel_id=1, source_target_pairs={{0,5},{1,4},{2,7},{3,6},{4,1},{5,0},{6,3},{7,2},{8,13},{9,12},{10,... | collective-permute-start | bytes 196616 | tf_op jit(solution)/shard_map/ppermute | solution.py:197
  2.5 0.7 %collective-permute-start = (bf16[4,16,4,128]{3,2,1,0:T(4,128)(2,1)}, bf16[4,16,4,128]{3,2,1,0:T(4,128)(2,1)S(1)}, u32[]{:S(2)}, u32[]{:S(2)}) collective-permute-start(bf16[4,16,4,128]{3,2,1,0:T(4,128)(2,1)} %param.8), channel_id=1, source_target_pairs={{0,4},{1,5},{2,6},{3,7},{4,0},{5,1},{6,2},{7,3},{8,12},{9,13},{10,... | collective-permute-start | bytes 196616 | tf_op jit(solution)/shard_map/ppermute | solution.py:197
  3.2 0.0 copy-start
  3.2 0.0 collective-permute-start.3
  3.2 1.4 %collective-permute-done.3.far_ref = bf16[1,2,3,2,128]{4,3,2,1,0:T(2,128)(2,1)S(1)} collective-permute-done((bf16[1,2,3,2,128]{4,3,2,1,0:T(2,128)(2,1)}, bf16[1,2,3,2,128]{4,3,2,1,0:T(2,128)(2,1)S(1)}, u32[]{:S(2)}, u32[]{:S(2)}) %collective-permute-start.3) | collective-permute-done | bytes 3104 | tf_op jit(solution)/shard_map/ppermute | solution.py:197
  4.5 0.0 copy-start.4
  4.5 0.7 %copy-done.4 = bf16[2,3,2,128]{3,2,1,0:T(2,128)(2,1)S(1)} copy-done((bf16[2,3,2,128]{3,2,1,0:T(2,128)(2,1)S(1)}, bf16[2,3,2,128]{3,2,1,0:T(2,128)(2,1)}, u32[]{:S(2)}) %copy-start.4) | copy-done | bytes 3096
  5.2 1.5 %collective-permute-start.5 = (bf16[2,2,3,2,128]{4,3,2,1,0:T(2,128)(2,1)S(1)}, bf16[2,2,3,2,128]{4,3,2,1,0:T(2,128)(2,1)S(1)}, u32[]{:S(2)}, u32[]{:S(2)}) collective-permute-start(bf16[2,2,3,2,128]{4,3,2,1,0:T(2,128)(2,1)S(1)} %shard_map.64.refs_0_), channel_id=1, source_target_pairs={{0,16},{1,17},{2,18},{3,19},{4,28},{5,29},{6,30},{7,31},{8,24},{9,... | collective-permute-start | bytes 18440 | tf_op jit(solution)/shard_map/ppermute | solution.py:197
  6.8 0.0 copy-done
  6.8 0.9 %collective-permute-start.2 = (bf16[2,3,4,128]{3,2,1,0:T(4,128)(2,1)S(1)}, bf16[2,3,4,128]{3,2,1,0:T(4,128)(2,1)S(1)}, u32[]{:S(2)}, u32[]{:S(2)}) collective-permute-start(bf16[2,3,4,128]{3,2,1,0:T(4,128)(2,1)S(1)} %copy-done), channel_id=1, source_target_pairs={{0,5},{1,4},{2,7},{3,6},{4,1},{5,0},{6,3},{7,2},{8,13},{9,12},{10,... | collective-permute-start | bytes 18440 | tf_op jit(solution)/shard_map/ppermute | solution.py:197
  7.6 0.8 %collective-permute-start.4 = (bf16[2,2,3,2,128]{4,3,2,1,0:T(2,128)(2,1)S(1)}, bf16[2,2,3,2,128]{4,3,2,1,0:T(2,128)(2,1)S(1)}, u32[]{:S(2)}, u32[]{:S(2)}) collective-permute-start(bf16[2,2,3,2,128]{4,3,2,1,0:T(2,128)(2,1)S(1)} %shard_map.64.refs_0_), channel_id=1, source_target_pairs={{0,12},{1,13},{2,14},{3,15},{4,8},{5,9},{6,10},{7,11},{8,4},{9,5},... | collective-permute-start | bytes 18440 | tf_op jit(solution)/shard_map/ppermute | solution.py:197
  8.4 0.4 %collective-permute-done.5.refs_1_ = bf16[2,2,3,2,128]{4,3,2,1,0:T(2,128)(2,1)S(1)} collective-permute-done((bf16[2,2,3,2,128]{4,3,2,1,0:T(2,128)(2,1)S(1)}, bf16[2,2,3,2,128]{4,3,2,1,0:T(2,128)(2,1)S(1)}, u32[]{:S(2)}, u32[]{:S(2)}) %collective-permute-start.5) | collective-permute-done | bytes 6176 | tf_op jit(solution)/shard_map/ppermute | solution.py:197
  8.9 0.0 collective-permute-start.6
  8.9 0.9 %collective-permute-done.2.beam_far_ref = bf16[2,3,4,128]{3,2,1,0:T(4,128)(2,1)S(1)} collective-permute-done((bf16[2,3,4,128]{3,2,1,0:T(4,128)(2,1)S(1)}, bf16[2,3,4,128]{3,2,1,0:T(4,128)(2,1)S(1)}, u32[]{:S(2)}, u32[]{:S(2)}) %collective-permute-start.2) | collective-permute-done | bytes 6176 | tf_op jit(solution)/shard_map/ppermute | solution.py:197
  9.8 0.0 collective-permute-done.1.table_far_ref
  9.8 0.0 collective-permute-done.table_ref
  9.8 0.1 shard_map.65.refs_2_
  10.0 0.7 %collective-permute-done.4.refs_0_ = bf16[2,2,3,2,128]{4,3,2,1,0:T(2,128)(2,1)S(1)} collective-permute-done((bf16[2,2,3,2,128]{4,3,2,1,0:T(2,128)(2,1)S(1)}, bf16[2,2,3,2,128]{4,3,2,1,0:T(2,128)(2,1)S(1)}, u32[]{:S(2)}, u32[]{:S(2)}) %collective-permute-start.4) | collective-permute-done | bytes 6176 | tf_op jit(solution)/shard_map/ppermute | solution.py:197
  10.7 0.0 collective-permute-done.6.refs_1_
  10.7 0.0 copy-start.3
  10.7 0.2 %shard_map.66 = f32[16,128]{1,0:T(8,128)S(1)} custom-call(s32[1]{0:T(128)} %bitcast.place_ref, bf16[4,16,4,128]{3,2,1,0:T(4,128)(2,1)S(1)} %collective-permute-done.table_ref, bf16[4,16,4,128]{3,2,1,0:T(4,128)(2,1)S(1)} %collective-permute-done.1.table_far_ref, bf16[2,3,4,128]{3,2,1,0:T(4,128)(2,1)S(1)} %copy-done, ...), custom_call_target="tpu_custom_call" | custom-call | tf_op jit(solution)/shard_map/pallas_call | solution.py:23
  10.9 2.5 %collective-permute-start.8 = (f32[16,128]{1,0:T(8,128)S(1)}, f32[16,128]{1,0:T(8,128)S(1)}, u32[]{:S(2)}, u32[]{:S(2)}) collective-permute-start(f32[16,128]{1,0:T(8,128)S(1)} %shard_map.66), channel_id=1, source_target_pairs={{0,6},{1,7},{2,4},{3,5},{4,2},{5,3},{6,0},{7,1},{8,14},{9,15},{10,... | collective-permute-start | bytes 24584 | tf_op jit(solution)/shard_map/ppermute | solution.py:197
  13.4 0.2 %collective-permute-start.7 = (f32[16,128]{1,0:T(8,128)S(1)}, f32[16,128]{1,0:T(8,128)S(1)}, u32[]{:S(2)}, u32[]{:S(2)}) collective-permute-start(f32[16,128]{1,0:T(8,128)S(1)} %shard_map.66), channel_id=1, source_target_pairs={{0,4},{1,5},{2,6},{3,7},{4,0},{5,1},{6,2},{7,3},{8,12},{9,13},{10,... | collective-permute-start | bytes 24584 | tf_op jit(solution)/shard_map/ppermute | solution.py:197
  13.6 0.0 copy-start.1
  13.6 0.0 copy-start.2
  13.7 0.0 copy-done.3
  13.7 0.7 %copy-done.1 = s32[16,256]{1,0:T(8,128)S(1)} copy-done((s32[16,256]{1,0:T(8,128)S(1)}, s32[16,256]{1,0:T(8,128)}, u32[]{:S(2)}) %copy-start.1) | copy-done | bytes 16408
  14.4 0.0 copy-done.2
  14.4 0.5 %shard_map.68 = (f32[16,1024]{1,0:T(8,128)S(1)}, f32[16,1024]{1,0:T(8,128)S(1)}, bf16[256,1024]{1,0:T(8,128)(2,1)S(1)}) custom-call(s32[1]{0:T(128)} %bitcast.4.own_ref, s32[16,256]{1,0:T(8,128)S(1)} %copy-done.1, s32[16,256]{1,0:T(8,128)S(1)} %copy-done.2, s32[16,256]{1,0:T(8,128)S(1)} %copy-done.3, s32[16,128]{1,0:T(8,128)S(1)} %shard_map.67.plane_ref), custom_call_target="tpu_custom_call" | custom-call | tf_op jit(solution)/shard_map/pallas_call | solution.py:23
  14.8 0.1 collective-permute-done.8
  14.9 0.0 collective-permute-done.7
  14.9 0.3 %shard_map.69 = (f32[8,64]{1,0:T(8,128)S(1)}, f32[8,64]{1,0:T(8,128)S(1)}) custom-call(f32[1,16,128]{2,1,0:T(8,128)S(1)} %bitcast.6, f32[1,16,128]{2,1,0:T(8,128)S(1)} %bitcast.5, f32[16,1024]{1,0:T(8,128)S(1)} %get-tuple-element.10.cos_ref, f32[16,1024]{1,0:T(8,128)S(1)} %get-tuple-element.11.sin_ref, bf16[256,1024]{1,0:T(8,128)(2,1)S(1)} %get-tuple-element.12.factor_ref), custom_call_target="tpu_custom_call" | custom-call | tf_op jit(solution)/shard_map/pallas_call | solution.py:23
  15.2 0.6 %pad_maximum_fusion = f32[16,64]{1,0:T(8,128)} fusion(f32[8,64]{1,0:T(8,128)S(1)} %get-tuple-element.14, f32[8,64]{1,0:T(8,128)S(1)} %get-tuple-element.13), kind=kLoop, calls=%fused_computation | loop fusion | flops 1024 | bytes 8192 | tf_op jit(solution)/shard_map/concatenate | solution.py:253
  (2 shorter events, 0.0 us)
Async XLA Ops:
  0.0 9.8 %collective-permute-start.1 = (bf16[4,16,4,128]{3,2,1,0:T(4,128)(2,1)}, bf16[4,16,4,128]{3,2,1,0:T(4,128)(2,1)S(1)}, u32[]{:S(2)}, u32[]{:S(2)}) collective-permute-start(bf16[4,16,4,128]{3,2,1,0:T(4,128)(2,1)} %param.8), channel_id=1, source_target_pairs={{0,5},{1,4},{2,7},{3,6},{4,1},{5,0},{6,3},{7,2},{8,13},{9,12},{10,... | collective-permute-start | bytes 196616 | tf_op jit(solution)/shard_map/ppermute | solution.py:197
  2.5 7.3 %collective-permute-start = (bf16[4,16,4,128]{3,2,1,0:T(4,128)(2,1)}, bf16[4,16,4,128]{3,2,1,0:T(4,128)(2,1)S(1)}, u32[]{:S(2)}, u32[]{:S(2)}) collective-permute-start(bf16[4,16,4,128]{3,2,1,0:T(4,128)(2,1)} %param.8), channel_id=1, source_target_pairs={{0,4},{1,5},{2,6},{3,7},{4,0},{5,1},{6,2},{7,3},{8,12},{9,13},{10,... | collective-permute-start | bytes 196616 | tf_op jit(solution)/shard_map/ppermute | solution.py:197
  3.2 3.6 %copy-start = (bf16[2,3,4,128]{3,2,1,0:T(4,128)(2,1)S(1)}, bf16[2,3,4,128]{3,2,1,0:T(4,128)(2,1)}, u32[]{:S(2)}) copy-start(bf16[2,3,4,128]{3,2,1,0:T(4,128)(2,1)} %beam_ref.3) | copy-start | bytes 18436
  3.2 1.4 %collective-permute-start.3 = (bf16[1,2,3,2,128]{4,3,2,1,0:T(2,128)(2,1)}, bf16[1,2,3,2,128]{4,3,2,1,0:T(2,128)(2,1)S(1)}, u32[]{:S(2)}, u32[]{:S(2)}) collective-permute-start(bf16[1,2,3,2,128]{4,3,2,1,0:T(2,128)(2,1)} %bitcast.7), channel_id=1, source_target_pairs={{0,4},{1,5},{2,6},{3,7},{4,0},{5,1},{6,2},{7,3},{8,12},{9,13},{10,... | collective-permute-start | bytes 9224 | tf_op jit(solution)/shard_map/ppermute | solution.py:197
  4.5 0.7 %copy-start.4 = (bf16[2,3,2,128]{3,2,1,0:T(2,128)(2,1)S(1)}, bf16[2,3,2,128]{3,2,1,0:T(2,128)(2,1)}, u32[]{:S(2)}) copy-start(bf16[2,3,2,128]{3,2,1,0:T(2,128)(2,1)} %param.6) | copy-start | bytes 9220
  5.2 3.6 %collective-permute-start.5 = (bf16[2,2,3,2,128]{4,3,2,1,0:T(2,128)(2,1)S(1)}, bf16[2,2,3,2,128]{4,3,2,1,0:T(2,128)(2,1)S(1)}, u32[]{:S(2)}, u32[]{:S(2)}) collective-permute-start(bf16[2,2,3,2,128]{4,3,2,1,0:T(2,128)(2,1)S(1)} %shard_map.64.refs_0_), channel_id=1, source_target_pairs={{0,16},{1,17},{2,18},{3,19},{4,28},{5,29},{6,30},{7,31},{8,24},{9,... | collective-permute-start | bytes 18440 | tf_op jit(solution)/shard_map/ppermute | solution.py:197
  6.8 3.1 %collective-permute-start.2 = (bf16[2,3,4,128]{3,2,1,0:T(4,128)(2,1)S(1)}, bf16[2,3,4,128]{3,2,1,0:T(4,128)(2,1)S(1)}, u32[]{:S(2)}, u32[]{:S(2)}) collective-permute-start(bf16[2,3,4,128]{3,2,1,0:T(4,128)(2,1)S(1)} %copy-done), channel_id=1, source_target_pairs={{0,5},{1,4},{2,7},{3,6},{4,1},{5,0},{6,3},{7,2},{8,13},{9,12},{10,... | collective-permute-start | bytes 18440 | tf_op jit(solution)/shard_map/ppermute | solution.py:197
  7.6 3.1 %collective-permute-start.4 = (bf16[2,2,3,2,128]{4,3,2,1,0:T(2,128)(2,1)S(1)}, bf16[2,2,3,2,128]{4,3,2,1,0:T(2,128)(2,1)S(1)}, u32[]{:S(2)}, u32[]{:S(2)}) collective-permute-start(bf16[2,2,3,2,128]{4,3,2,1,0:T(2,128)(2,1)S(1)} %shard_map.64.refs_0_), channel_id=1, source_target_pairs={{0,12},{1,13},{2,14},{3,15},{4,8},{5,9},{6,10},{7,11},{8,4},{9,5},... | collective-permute-start | bytes 18440 | tf_op jit(solution)/shard_map/ppermute | solution.py:197
  8.9 1.8 %collective-permute-start.6 = (bf16[2,2,3,2,128]{4,3,2,1,0:T(2,128)(2,1)S(1)}, bf16[2,2,3,2,128]{4,3,2,1,0:T(2,128)(2,1)S(1)}, u32[]{:S(2)}, u32[]{:S(2)}) collective-permute-start(bf16[2,2,3,2,128]{4,3,2,1,0:T(2,128)(2,1)S(1)} %collective-permute-done.5.refs_1_), channel_id=1, source_target_pairs={{0,4},{1,5},{2,6},{3,7},{4,0},{5,1},{6,2},{7,3},{8,12},{9,13},{10,... | collective-permute-start | bytes 18440 | tf_op jit(solution)/shard_map/ppermute | solution.py:197
  10.7 3.0 %copy-start.3 = (s32[16,256]{1,0:T(8,128)S(1)}, s32[16,256]{1,0:T(8,128)}, u32[]{:S(2)}) copy-start(s32[16,256]{1,0:T(8,128)} %psi_ref.1) | copy-start | bytes 49156
  10.9 4.0 %collective-permute-start.8 = (f32[16,128]{1,0:T(8,128)S(1)}, f32[16,128]{1,0:T(8,128)S(1)}, u32[]{:S(2)}, u32[]{:S(2)}) collective-permute-start(f32[16,128]{1,0:T(8,128)S(1)} %shard_map.66), channel_id=1, source_target_pairs={{0,6},{1,7},{2,4},{3,5},{4,2},{5,3},{6,0},{7,1},{8,14},{9,15},{10,... | collective-permute-start | bytes 24584 | tf_op jit(solution)/shard_map/ppermute | solution.py:197
  13.4 1.5 %collective-permute-start.7 = (f32[16,128]{1,0:T(8,128)S(1)}, f32[16,128]{1,0:T(8,128)S(1)}, u32[]{:S(2)}, u32[]{:S(2)}) collective-permute-start(f32[16,128]{1,0:T(8,128)S(1)} %shard_map.66), channel_id=1, source_target_pairs={{0,4},{1,5},{2,6},{3,7},{4,0},{5,1},{6,2},{7,3},{8,12},{9,13},{10,... | collective-permute-start | bytes 24584 | tf_op jit(solution)/shard_map/ppermute | solution.py:197
  13.6 0.7 %copy-start.1 = (s32[16,256]{1,0:T(8,128)S(1)}, s32[16,256]{1,0:T(8,128)}, u32[]{:S(2)}) copy-start(s32[16,256]{1,0:T(8,128)} %theta_ref.1) | copy-start | bytes 49156
  13.6 0.7 %copy-start.2 = (s32[16,256]{1,0:T(8,128)S(1)}, s32[16,256]{1,0:T(8,128)}, u32[]{:S(2)}) copy-start(s32[16,256]{1,0:T(8,128)} %phi_ref.1) | copy-start | bytes 49156
